TPU v7x, 512 devices: a whole 4x8x8 slice. The times are simulated.
512 devices in a mesh: node: 64 (over z, y), harm: 8 (over x, core).
Axes of the slice: x: 4, y: 8, z: 8, core: 2. Of those that a mesh axis runs over, the one named last changes fastest.
Arguments:
- spectrum: float32 [128, 3, 393216], P('harm', None, 'node'), may hold values from -2 to 2
- source: float32 [128, 3, 393216], P('harm', None, 'node'), may hold values from -4 to 4
- coupling: bfloat16 [3072, 4, 128, 128], P('node'), may hold values from -0.75 to 0.75
- capacitance: float32 [393216], P('node'), may hold values from 0.5 to 4
- saturation: float32 [393216], P('node'), may hold values from 0.1 to 1
- steepness: float32 [393216], P('node'), may hold values from 0.5 to 4
- junction: float32 [393216], P('node'), may hold values from 0.2 to 2
- halo_list: int32 [64, 4, 4], replicated, may hold values from 0 to 47, as said below
- neighbour_slot: int32 [3072, 4], P('node'), may hold values from 0 to 64, as said below
Outputs:
- residual: float32 [128, 3, 393216], P('harm', None, 'node')
Inputs may be any that keep to these rules, and one draw needn't show every extreme that they name: `halo_list`: row [m, j] lists 4 distinct blocks of device m, by index among its 48 blocks, needed by the device at index m + o_j along node, o = (-2, -1, 1, 2). `neighbour_slot`: column 0 of block b is b's own index among the 48 blocks of its device d. Other entries v: own block v if v < 48; block halo_list[m, j, s] of device m = d - o_j if v = 48 + j * 4 + s, only where m lies on the mesh; v = 64 is an empty entry. Every such slot of a device whose sender lies on the mesh is named by some entry of the device.
All inputs are finite; a program needn't handle non-finite values.
Results may differ from a plain program's by a relative error of at most 0.0025.
Values may be sent and summed in bfloat16 or wider, within the bound.
A program may use at most 64 MiB of HBM per device.

v0:
```python
import jax
import jax.numpy as jnp
from jax import lax
from jax.sharding import Mesh
from jax.sharding import PartitionSpec as P

HARM = ("harm_0", "harm_1")


LOG_TWO = 0.6931471805599453
OFFSETS = (-2, -1, 1, 2)


def passed_along(value, axis, by):
    length = lax.axis_size(axis)
    pairs = [(i, i + by) for i in range(length) if 0 <= i + by < length]
    return lax.ppermute(value, axis, pairs)


def cut_along(value, dim, length):
    dims = value.shape
    blocks = value.reshape(*dims[:dim], length, dims[dim] // length, *dims[dim + 1 :])
    return jnp.moveaxis(blocks, dim, 0)


def joined_along(blocks, dim):
    dims = list(blocks.shape[1:])
    dims[dim] *= blocks.shape[0]
    return jnp.moveaxis(blocks, 0, dim).reshape(dims)


def exchange_in_order(blocks, axes, sequence):
    inside = blocks.shape[1:]
    whole = blocks.reshape(*(lax.axis_size(a) for a in axes), *inside)
    for k in sequence:
        whole = lax.all_to_all(whole, axes[k], k, k, tiled=True)
    return whole.reshape(-1, *inside)


def exchange_by_chip(value, groups, sequence, split_dim, concat_dim):
    length = lax.axis_size(groups[0]) * lax.axis_size(groups[1])
    blocks = cut_along(value, split_dim, length)
    return joined_along(exchange_in_order(blocks, groups, sequence), concat_dim)


def synthesis_table(length):
    sample = jnp.arange(length, dtype=jnp.int32)[:, None]
    column = jnp.arange(length, dtype=jnp.int32)[None, :]
    phase = column // 2 * sample % length
    angle_value = 2.0 * jnp.pi / length * phase.astype(jnp.float32)
    table_value = jnp.where(column % 2 == 1, jnp.sin(angle_value), jnp.cos(angle_value))
    alternate = jnp.where(sample % 2 == 0, 1.0, -1.0)
    return jnp.where(column == 1, alternate, table_value)


def derivative(values, first_row, harmonics):
    pairs = values.shape[0] // 2
    pulsation = (first_row // 2 + jnp.arange(pairs, dtype=jnp.int32)).astype(
        jnp.float32
    ) / harmonics
    pulsation = pulsation.reshape((pairs,) + (1,) * (values.ndim - 1))
    shaped = values.reshape((pairs, 2) + values.shape[1:])
    result = jnp.stack([pulsation * shaped[:, 1], -pulsation * shaped[:, 0]], axis=1)
    return result.reshape(values.shape)


def product(left, right):
    flat = right.reshape(right.shape[0], -1)
    outcome = jnp.dot(left, flat, preferred_element_type=jnp.float32)
    return outcome.reshape((left.shape[0],) + right.shape[1:])


def local(
    spectrum,
    source,
    coupling,
    capacitance,
    saturation,
    steepness,
    junction,
    halo_list,
    neighbour_slot,
):
    spec_rows, points, node_count = spectrum.shape
    whole_rows = spec_rows * lax.axis_size(HARM)
    harmonics = whole_rows // 2
    first_row = lax.axis_index(HARM) * spec_rows
    node_index = lax.axis_index("node")
    block_count = neighbour_slot.shape[0]
    block_size = node_count // block_count
    rounded = spectrum.astype(jnp.bfloat16)
    own_blocks = rounded.reshape(spec_rows, points, block_count, block_size)
    buffers = [own_blocks]
    for direction, offset in enumerate(OFFSETS):
        shard_copy = passed_along(rounded, "node", offset)
        sender = jnp.clip(node_index - offset, 0, lax.axis_size("node") - 1)
        listed = halo_list[sender, direction]
        buffers.append(shard_copy.reshape(spec_rows, points, block_count, block_size)[:, :, listed])
    buffers.append(jnp.zeros((spec_rows, points, 1, block_size), jnp.bfloat16))
    gathered = jnp.concatenate(buffers, axis=2)[:, :, neighbour_slot]
    coupled = jnp.einsum("spbkj,bkij->spbi", gathered, coupling, preferred_element_type=jnp.float32)
    coupled = coupled.reshape(spec_rows, points, node_count)
    synthesis = synthesis_table(whole_rows)
    weights = jnp.where(jnp.arange(whole_rows) < 2, 1.0 / whole_rows, 2.0 / whole_rows)
    analysis = synthesis.T * weights[:, None]
    columns = exchange_by_chip(
        spectrum.astype(jnp.bfloat16), ("harm_0", "harm_1"), (1, 0), 2, 0
    ).astype(spectrum.dtype)
    column_count = columns.shape[2]
    column_start = lax.axis_index(HARM) * column_count

    def select(values):
        return lax.dynamic_slice_in_dim(values, column_start, column_count, 0)

    voltage = product(synthesis, columns)
    current = select(saturation) * (jax.nn.softplus(select(steepness) * voltage) - LOG_TWO)
    charge = select(junction) * voltage / jnp.sqrt(1.0 + voltage * voltage)
    current_spec = product(analysis, current)
    charge_spec = product(analysis, charge)
    combined = current_spec + derivative(charge_spec, 0, harmonics)
    nonlinear = lax.all_to_all(
        combined.astype(jnp.bfloat16), HARM, split_axis=0, concat_axis=2, tiled=True
    ).astype(combined.dtype)
    residual = (
        coupled + derivative(capacitance * spectrum, first_row, harmonics) + nonlinear - source
    )
    return residual


def solution(mesh):
    split = Mesh(mesh.devices.reshape(mesh.shape["node"], 4, 2), ("node", "harm_0", "harm_1"))
    return jax.shard_map(
        local,
        mesh=split,
        in_specs=(
            P(HARM, None, "node"),
            P(HARM, None, "node"),
            P("node", None, None, None),
            P("node"),
            P("node"),
            P("node"),
            P("node"),
            P(),
            P("node", None),
        ),
        out_specs=P(HARM, None, "node"),
        check_vma=False,
    )
```

profile of v0, /device:TPU:279, one launch (start us, length us, event | category | flops | bytes accessed | tf_op | source)
XLA Modules:
  0.0 76.0 jit_solution(7047194970531401120)
XLA Ops:
  0.0 2.8 %broadcast_multiply_fusion = (f32[16,3,6144]{2,0,1:T(8,128)}, bf16[16,3,6144]{2,0,1:T(8,128)(2,1)S(1)}) fusion(f32[16,3,6144]{2,0,1:T(8,128)} %param.9, f32[6144]{0:T(1024)} %param.12), kind=kLoop, calls=%fused_computation.32 | loop fusion | flops 589824 | bytes 2973696 | tf_op jit(solution)/shard_map/mul | solution.py:125
  2.8 5.4 %collective-permute-start.3 = (bf16[16,3,6144]{2,0,1:T(8,128)(2,1)S(1)}, bf16[16,3,6144]{2,0,1:T(8,128)(2,1)}, u32[]{:S(2)}, u32[]{:S(2)}) collective-permute-start(bf16[16,3,6144]{2,0,1:T(8,128)(2,1)S(1)} %get-tuple-element.12), channel_id=1, source_target_pairs={{0,16},{8,24},{16,32},{24,40},{32,48},{40,56},{48,64},{56,72},{64,... | collective-permute-start | bytes 1769480 | tf_op jit(solution)/shard_map/ppermute | solution.py:17
  8.2 2.3 %collective-permute-start.2 = (bf16[16,3,6144]{2,0,1:T(8,128)(2,1)S(1)}, bf16[16,3,6144]{2,0,1:T(8,128)(2,1)}, u32[]{:S(2)}, u32[]{:S(2)}) collective-permute-start(bf16[16,3,6144]{2,0,1:T(8,128)(2,1)S(1)} %get-tuple-element.12), channel_id=1, source_target_pairs={{0,8},{8,16},{16,24},{24,32},{32,40},{40,48},{48,56},{56,64},{64,7... | collective-permute-start | bytes 1769480 | tf_op jit(solution)/shard_map/ppermute | solution.py:17
  10.5 3.0 %collective-permute-start.1 = (bf16[16,3,6144]{2,0,1:T(8,128)(2,1)S(1)}, bf16[16,3,6144]{2,0,1:T(8,128)(2,1)}, u32[]{:S(2)}, u32[]{:S(2)}) collective-permute-start(bf16[16,3,6144]{2,0,1:T(8,128)(2,1)S(1)} %get-tuple-element.12), channel_id=1, source_target_pairs={{8,0},{16,8},{24,16},{32,24},{40,32},{48,40},{56,48},{64,56},{72,6... | collective-permute-start | bytes 1769480 | tf_op jit(solution)/shard_map/ppermute | solution.py:17
  13.5 4.1 %collective-permute-start = (bf16[16,3,6144]{2,0,1:T(8,128)(2,1)S(1)}, bf16[16,3,6144]{2,0,1:T(8,128)(2,1)}, u32[]{:S(2)}, u32[]{:S(2)}) collective-permute-start(bf16[16,3,6144]{2,0,1:T(8,128)(2,1)S(1)} %get-tuple-element.12), channel_id=1, source_target_pairs={{16,0},{24,8},{32,16},{40,24},{48,32},{56,40},{64,48},{72,56},{80,... | collective-permute-start | bytes 1769480 | tf_op jit(solution)/shard_map/ppermute | solution.py:17
  17.9 5.6 %all_to_all.19 = bf16[4,2,16,3,768]{4,2,3,0,1:T(8,128)(2,1)S(1)} all-to-all(bf16[4,2,16,3,768]{4,2,3,0,1:T(8,128)(2,1)S(1)} %copy.98), channel_id=1, replica_groups=mesh['node'=64,'harm_0'=4,'harm_1'=2] {'harm_1'}, dimensions={1} | all-to-all | bytes 1179648 | tf_op jit(solution)/shard_map/all_to_all | solution.py:36
  24.4 4.2 %all-to-all-start.1 = ((bf16[4,2,16,3,768]{4,2,3,1,0:T(8,128)(2,1)}), bf16[4,2,16,3,768]{4,2,3,1,0:T(8,128)(2,1)S(1)}, u32[]{:S(2)}, u32[]{:S(2)}) async-start(bf16[4,2,16,3,768]{4,2,3,1,0:T(8,128)(2,1)} %copy.99), calls=%async_computation.1 | async-start | bytes 1179648 | tf_op jit(solution)/shard_map/all_to_all | solution.py:36
  31.6 2.0 %reshape.384 = f32[8,2,3,6144]{3,1,0,2:T(2,128)S(1)} reshape(f32[16,3,6144]{2,0,1:T(8,128)} %get-tuple-element.11) | data formatting | bytes 2359296 | tf_op jit(solution)/shard_map/reshape | solution.py:62
  34.4 1.1 %pad_maximum_fusion = f32[8,2,3,6144]{3,1,0,2:T(2,128)S(1)} fusion(f32[8,1,3,6144]{3,1,0,2:T(1,128)S(1)} %get-tuple-element.10, f32[8,1,3,6144]{3,1,0,2:T(1,128)S(1)} %get-tuple-element.9), kind=kLoop, calls=%fused_computation.16 | loop fusion | flops 294912 | bytes 2359296 | tf_op jit(solution)/shard_map/stack | solution.py:63
  35.5 1.8 %reshape.385 = f32[16,3,6144]{2,0,1:T(8,128)} reshape(f32[8,2,3,6144]{3,1,0,2:T(2,128)S(1)} %pad_maximum_fusion) | data formatting | bytes 2359296 | tf_op jit(solution)/shard_map/reshape | solution.py:64
  38.2 2.1 %fusion.7 = (bf16[128,3,768]{2,0,1:T(8,128)(2,1)}, bf16[128,3,768]{2,0,1:T(8,128)(2,1)S(1)}) fusion(f32[768]{0:T(1024)S(1)} %dynamic_slice.26, f32[768]{0:T(1024)S(1)} %dynamic_slice.25, f32[768]{0:T(1024)S(1)} %dynamic_slice.27, bf16[3,768,128]{2,1,0:T(8,128)(2,1)S(1)} %bitcast.148, s32[128]{0:T(128)S(1)} %and_select_fusion.2, ...), kind=kOutput, calls=%fused_computation.12 | convolution fusion | flops 80183296 | bytes 1779968 | tf_op jit(solution)/shard_map/dot_general | solution.py:69
  41.6 1.4 %copy.102 = bf16[128,3,768]{0,2,1:T(8,128)(2,1)S(1)} copy(bf16[128,3,768]{2,0,1:T(8,128)(2,1)} %get-tuple-element.13) | data formatting | bytes 1179648 | tf_op jit(solution)/shard_map/mul | solution.py:116
  42.9 1.9 %copy.104 = f32[64,2,3,768]{3,1,0,2:T(2,128)} copy(f32[64,2,3,768]{3,0,2,1:T(8,128)S(1)} %pad_maximum_fusion.1) | data formatting | bytes 2359296 | tf_op jit(solution)/shard_map/stack | solution.py:63
  44.9 2.1 %reshape.391 = f32[128,3,768]{2,0,1:T(8,128)S(1)} reshape(f32[64,2,3,768]{3,1,0,2:T(2,128)} %copy.104) | data formatting | bytes 2359296 | tf_op jit(solution)/shard_map/reshape | solution.py:64
  47.6 1.4 %copy.105 = bf16[128,3,768]{2,1,0:T(4,128)(2,1)} copy(bf16[128,3,768]{2,0,1:T(8,128)(2,1)S(1)} %fusion.5) | data formatting | bytes 1179648 | tf_op jit(solution)/shard_map/convert_element_type | solution.py:122
  49.0 6.3 %all-to-all-start.2 = ((bf16[128,3,768]{2,1,0:T(4,128)(2,1)}), bf16[128,3,768]{2,1,0:T(4,128)(2,1)}, u32[]{:S(2)}, u32[]{:S(2)}) async-start(bf16[128,3,768]{2,1,0:T(4,128)(2,1)} %copy.105), calls=%async_computation.2 | async-start | bytes 1572864 | tf_op jit(solution)/shard_map/all_to_all | solution.py:121
  55.3 1.2 %copy_bitcast_fusion.1 = bf16[16,3,48,128]{3,0,2,1:T(8,128)(2,1)S(1)} fusion(bf16[16,3,6144]{2,0,1:T(8,128)(2,1)} %collective-permute-done.3), kind=kLoop, calls=%fused_computation.23 | loop fusion | bytes 1179648 | tf_op jit(solution)/shard_map/reshape | solution.py:98
  57.0 1.2 %copy_bitcast_fusion.2 = bf16[16,3,48,128]{3,0,2,1:T(8,128)(2,1)S(1)} fusion(bf16[16,3,6144]{2,0,1:T(8,128)(2,1)} %collective-permute-done.2), kind=kLoop, calls=%fused_computation.24 | loop fusion | bytes 1179648 | tf_op jit(solution)/shard_map/reshape | solution.py:98
  58.8 1.2 %copy_bitcast_fusion.3 = bf16[16,3,48,128]{3,0,2,1:T(8,128)(2,1)S(1)} fusion(bf16[16,3,6144]{2,0,1:T(8,128)(2,1)} %collective-permute-done.1), kind=kLoop, calls=%fused_computation.25 | loop fusion | bytes 1179648 | tf_op jit(solution)/shard_map/reshape | solution.py:98
  60.5 1.2 %copy_bitcast_fusion.4 = bf16[16,3,48,128]{3,0,2,1:T(8,128)(2,1)S(1)} fusion(bf16[16,3,6144]{2,0,1:T(8,128)(2,1)} %collective-permute-done), kind=kLoop, calls=%fused_computation.26 | loop fusion | bytes 1179648 | tf_op jit(solution)/shard_map/reshape | solution.py:98
  63.4 6.1 %fusion.2 = f32[48,3,2,8,128]{4,3,2,1,0:T(8,128)} fusion(bf16[16,3,48,4,128]{4,0,1,3,2:T(8,128)(2,1)S(1)} %bitcast.141, bf16[48,4,128,128]{3,2,1,0:T(8,128)(2,1)} %param.11), kind=kOutput, calls=%fused_computation.8 | convolution fusion | flops 301989888 | bytes 9830400 | tf_op jit(solution)/shard_map/spbkj,bkij->spbi/dot_general | solution.py:101
  69.5 1.6 %copy.129 = f32[8,16,3,768]{3,0,1,2:T(8,128)S(1)} copy(bf16[8,16,3,768]{3,2,1,0:T(4,128)(2,1)} %bitcast.42) | data formatting | bytes 1769472 | tf_op jit(solution)/shard_map/convert_element_type | solution.py:123
  71.1 1.2 %reshape.392 = f32[16,3,6144]{2,0,1:T(8,128)} reshape(f32[16,3,8,768]{3,2,0,1:T(8,128)S(1)} %bitcast.143) | data formatting | bytes 2359296 | tf_op jit(solution)/shard_map/convert_element_type | solution.py:123
  73.1 2.9 %fusion.9 = f32[16,3,6144]{2,0,1:T(8,128)} fusion(f32[16,3,6144]{2,0,1:T(8,128)} %param.10, f32[16,3,6144]{2,0,1:T(8,128)} %reshape.392, f32[16,3,6144]{2,0,1:T(8,128)S(1)} %copy-done.1, f32[48,3,2,8,128]{4,3,2,1,0:T(8,128)S(1)} %copy-done), kind=kLoop, calls=%fused_computation.15 | loop fusion | flops 884736 | bytes 5898240 | tf_op jit(solution)/shard_map/sub | solution.py:125
  (62 shorter events, 11.7 us)
Async XLA Ops:
  2.8 52.5 %collective-permute-start.3 = (bf16[16,3,6144]{2,0,1:T(8,128)(2,1)S(1)}, bf16[16,3,6144]{2,0,1:T(8,128)(2,1)}, u32[]{:S(2)}, u32[]{:S(2)}) collective-permute-start(bf16[16,3,6144]{2,0,1:T(8,128)(2,1)S(1)} %get-tuple-element.12), channel_id=1, source_target_pairs={{0,16},{8,24},{16,32},{24,40},{32,48},{40,56},{48,64},{56,72},{64,... | collective-permute-start | bytes 1769480 | tf_op jit(solution)/shard_map/ppermute | solution.py:17
  8.2 48.8 %collective-permute-start.2 = (bf16[16,3,6144]{2,0,1:T(8,128)(2,1)S(1)}, bf16[16,3,6144]{2,0,1:T(8,128)(2,1)}, u32[]{:S(2)}, u32[]{:S(2)}) collective-permute-start(bf16[16,3,6144]{2,0,1:T(8,128)(2,1)S(1)} %get-tuple-element.12), channel_id=1, source_target_pairs={{0,8},{8,16},{16,24},{24,32},{32,40},{40,48},{48,56},{56,64},{64,7... | collective-permute-start | bytes 1769480 | tf_op jit(solution)/shard_map/ppermute | solution.py:17
  10.5 48.3 %collective-permute-start.1 = (bf16[16,3,6144]{2,0,1:T(8,128)(2,1)S(1)}, bf16[16,3,6144]{2,0,1:T(8,128)(2,1)}, u32[]{:S(2)}, u32[]{:S(2)}) collective-permute-start(bf16[16,3,6144]{2,0,1:T(8,128)(2,1)S(1)} %get-tuple-element.12), channel_id=1, source_target_pairs={{8,0},{16,8},{24,16},{32,24},{40,32},{48,40},{56,48},{64,56},{72,6... | collective-permute-start | bytes 1769480 | tf_op jit(solution)/shard_map/ppermute | solution.py:17
  13.5 47.0 %collective-permute-start = (bf16[16,3,6144]{2,0,1:T(8,128)(2,1)S(1)}, bf16[16,3,6144]{2,0,1:T(8,128)(2,1)}, u32[]{:S(2)}, u32[]{:S(2)}) collective-permute-start(bf16[16,3,6144]{2,0,1:T(8,128)(2,1)S(1)} %get-tuple-element.12), channel_id=1, source_target_pairs={{16,0},{24,8},{32,16},{40,24},{48,32},{56,40},{64,48},{72,56},{80,... | collective-permute-start | bytes 1769480 | tf_op jit(solution)/shard_map/ppermute | solution.py:17
  23.5 5.2 %copy-start.2 = (s32[64,4,4]{0,2,1:T(4,128)S(1)}, s32[64,4,4]{0,2,1:T(4,128)}, u32[]{:S(2)}) copy-start(s32[64,4,4]{0,2,1:T(4,128)} %param.16) | copy-start | bytes 12292
  23.5 5.5 %copy-start.3 = (s32[48,4]{0,1:T(4,128)S(1)}, s32[48,4]{0,1:T(4,128)}, u32[]{:S(2)}) copy-start(s32[48,4]{0,1:T(4,128)} %param.17) | copy-start | bytes 2308
  24.4 13.1 %all-to-all-start.1 = ((bf16[4,2,16,3,768]{4,2,3,1,0:T(8,128)(2,1)}), bf16[4,2,16,3,768]{4,2,3,1,0:T(8,128)(2,1)S(1)}, u32[]{:S(2)}, u32[]{:S(2)}) async-start(bf16[4,2,16,3,768]{4,2,3,1,0:T(8,128)(2,1)} %copy.99), calls=%async_computation.1 | async-start | bytes 1179648 | tf_op jit(solution)/shard_map/all_to_all | solution.py:36
  49.0 20.5 %all-to-all-start.2 = ((bf16[128,3,768]{2,1,0:T(4,128)(2,1)}), bf16[128,3,768]{2,1,0:T(4,128)(2,1)}, u32[]{:S(2)}, u32[]{:S(2)}) async-start(bf16[128,3,768]{2,1,0:T(4,128)(2,1)} %copy.105), calls=%async_computation.2 | async-start | bytes 1572864 | tf_op jit(solution)/shard_map/all_to_all | solution.py:121
  71.1 1.6 %copy-start = (f32[48,3,2,8,128]{4,3,2,1,0:T(8,128)S(1)}, f32[48,3,2,8,128]{4,3,2,1,0:T(8,128)}, u32[]{:S(2)}) copy-start(f32[48,3,2,8,128]{4,3,2,1,0:T(8,128)} %fusion.2) | copy-start | bytes 3538948
  71.1 2.0 %copy-start.1 = (f32[16,3,6144]{2,0,1:T(8,128)S(1)}, f32[16,3,6144]{2,0,1:T(8,128)}, u32[]{:S(2)}) copy-start(f32[16,3,6144]{2,0,1:T(8,128)} %reshape.385) | copy-start | bytes 3538948
where the time goes:
time: 77 us; the launch traced here: 76 us
  local copies, waits for them, and re-layouts  27.2 us (35%)
  starting transfers between devices  25.3 us (33%)
  matrix products  9.49 us (12%)
  other arithmetic  7.93 us (10%)
  blocking collectives  5.63 us (7%)
    ppermute x4, starting transfers between devices, passed_along(): return lax.ppermute(value, axis, pairs)  14.8 us
    all_to_all x1, starting transfers between devices, local(): lax.all_to_all(combined.astype(jnp.bfloat16), HARM, split_axis=0, concat_...  6.3 us
    dot_general x1, matrix products, local(): jnp.einsum('spbkj,bkij->spbi', gathered, coupling, preferred_element_type...  6.09 us
    all_to_all x1, blocking collectives, exchange_in_order(): whole = lax.all_to_all(whole, axes[k], k, k, tiled=True)  5.63 us
    reshape x4, local copies, waits for them, and re-layouts, local(): shard_copy.reshape(spec_rows, points, block_count, block_size)[:, :, listed]  4.67 us
    all_to_all x1, starting transfers between devices, exchange_in_order(): whole = lax.all_to_all(whole, axes[k], k, k, tiled=True)  4.21 us
    reshape x2, local copies, waits for them, and re-layouts, derivative(): return result.reshape(values.shape)  3.92 us
    dot_general x3, matrix products, product(): outcome = jnp.dot(left, flat, preferred_element_type=jnp.float32)  3.4 us
  transfers between devices with their start and end apart: 6, of which 0 were waited for; matrix products, arithmetic and copies ran while one was open for 47% of the time, Pallas kernels for 0%

commit v1 on v0

v1 whole, which is shorter than its diff:
```python
import functools

import jax
import jax.numpy as jnp
import numpy as np
from jax import lax
from jax.experimental import pallas as pl
from jax.experimental.pallas import tpu as pltpu
from jax.sharding import PartitionSpec as P

OFFSETS = (-2, -1, 1, 2)
LOG2_E = 1.4426950408889634
LN_2 = 0.6931471805599453
MESH = pl.DeviceIdType.MESH
CHUNKS = 3
COUPLING_COPIES = 6


def tables(rows):
    time = np.arange(rows)[:, None]
    row = np.arange(rows)[None, :]
    phase = (row // 2) * time % rows
    angle = 2.0 * np.pi / rows * phase
    synthesis = np.where(row % 2 == 1, np.sin(angle), np.cos(angle))
    synthesis = np.where(row == 1, np.where(time % 2 == 0, 1.0, -1.0), synthesis)
    weights = np.where(np.arange(rows) < 2, 1.0 / rows, 2.0 / rows)
    analysis = synthesis.T * weights[:, None]
    pulsation = (np.arange(rows) // 2)[:, None] / (rows // 2)
    derived = np.empty_like(analysis)
    derived[0::2] = pulsation[0::2] * analysis[1::2]
    derived[1::2] = -pulsation[1::2] * analysis[0::2]
    return synthesis, np.concatenate([analysis, derived], axis=1)


def body(
    n_node,
    n_harm,
    halo_ref,
    slot_ref,
    spectrum_hbm,
    source_hbm,
    coupling_hbm,
    capacitance_ref,
    saturation_ref,
    steepness_ref,
    junction_ref,
    synthesis_ref,
    analysis_ref,
    out_ref,
    spectrum_ref,
    source_ref,
    coupling_ref,
    blocks_ref,
    halo_out_ref,
    halo_in_ref,
    columns_ref,
    back_ref,
    result_ref,
    load_sem,
    halo_send_sem,
    halo_recv_sem,
    there_send_sem,
    there_recv_sem,
    back_send_sem,
    back_recv_sem,
):
    node = lax.axis_index("node")
    harm = lax.axis_index("harm")
    points, spec_rows, _ = spectrum_ref.shape
    block_count, listed, block_size, _ = coupling_ref.shape
    share = block_count // n_harm
    piece = share // CHUNKS
    rows = n_harm * spec_rows
    slots = halo_out_ref.shape[0] // len(OFFSETS)
    neighbours = [lax.rem(node + offset + n_node, n_node) for offset in OFFSETS]

    barrier = pltpu.get_barrier_semaphore()
    for step in range(1, n_harm):
        pl.semaphore_signal(
            barrier, inc=1, device_id=(node, lax.rem(harm + step, n_harm)), device_id_type=MESH
        )
    for neighbour in neighbours:
        pl.semaphore_signal(barrier, inc=1, device_id=(neighbour, harm), device_id_type=MESH)

    load_spectrum = pltpu.make_async_copy(spectrum_hbm, spectrum_ref, load_sem.at[0])
    load_spectrum.start()
    load_source = pltpu.make_async_copy(source_hbm, source_ref, load_sem.at[1])
    per_copy = block_count // COUPLING_COPIES
    load_coupling = [
        pltpu.make_async_copy(
            coupling_hbm.at[pl.ds(i * per_copy, per_copy)],
            coupling_ref.at[pl.ds(i * per_copy, per_copy)],
            load_sem.at[2 + i],
        )
        for i in range(COUPLING_COPIES)
    ]
    for copy in load_coupling:
        copy.start()
    load_source.start()

    load_spectrum.wait()

    def columns_of(b):
        return pl.ds(pl.multiple_of(b * block_size, block_size), block_size)

    def round_block(b, carry):
        blocks_ref[b] = spectrum_ref[:, :, columns_of(b)].astype(jnp.bfloat16)
        return carry

    lax.fori_loop(0, block_count, round_block, 0, unroll=8)
    empty = block_count + len(OFFSETS) * slots
    blocks_ref[empty] = jnp.zeros(blocks_ref.shape[1:], jnp.bfloat16)
    for i in range(len(OFFSETS) * slots):
        halo_out_ref[i] = blocks_ref[halo_ref[i, node]]

    pl.semaphore_wait(barrier, n_harm - 1 + len(OFFSETS))

    halo = []
    for j in range(len(OFFSETS)):
        copy = pltpu.make_async_remote_copy(
            src_ref=halo_out_ref.at[pl.ds(j * slots, slots)],
            dst_ref=halo_in_ref.at[pl.ds(j * slots, slots)],
            send_sem=halo_send_sem.at[j],
            recv_sem=halo_recv_sem.at[j],
            device_id=(neighbours[j], harm),
            device_id_type=MESH,
        )
        copy.start()
        halo.append(copy)
    there = []
    for c in range(CHUNKS):
        for step in range(1, n_harm):
            peer = lax.rem(harm + step, n_harm)
            copy = pltpu.make_async_remote_copy(
                src_ref=blocks_ref.at[pl.ds(peer * share + c * piece, piece)],
                dst_ref=columns_ref.at[harm, pl.ds(c * piece, piece)],
                send_sem=there_send_sem.at[c, step - 1],
                recv_sem=there_recv_sem.at[c, step - 1],
                device_id=(node, peer),
                device_id_type=MESH,
            )
            copy.start()
            there.append(copy)
    columns_ref[harm] = blocks_ref[pl.ds(harm * share, share)]

    for copy in halo:
        copy.wait_recv()
    blocks_ref[pl.ds(block_count, len(OFFSETS) * slots)] = halo_in_ref[...]

    row_index = lax.broadcasted_iota(jnp.int32, (1, 8, block_size), 1)
    even = row_index % 2 == 0
    tiles = spec_rows // 8
    pulsations = []
    for i in range(tiles):
        harmonic = (harm * spec_rows + i * 8 + row_index) // 2
        value = harmonic.astype(jnp.float32) * (2.0 / rows)
        pulsations.append(jnp.where(even, value, -value))
    pulsation = jnp.concatenate(pulsations * points, axis=0)

    def couple(b, carry):
        gathered = jnp.concatenate(
            [
                blocks_ref[slot_ref[k, b]].reshape(points * spec_rows, block_size)
                for k in range(listed)
            ],
            axis=1,
        )
        matrix = jnp.concatenate([coupling_ref[b, k] for k in range(listed)], axis=1)
        coupled = lax.dot_general(
            gathered, matrix, (((1,), (1,)), ((), ())), preferred_element_type=jnp.float32
        )
        columns = columns_of(b)
        stored = capacitance_ref[pl.ds(b, 1)] * spectrum_ref[:, :, columns].reshape(
            points * spec_rows, block_size
        )
        stored = stored.reshape(points * tiles, 8, block_size)
        swapped = jnp.where(even, pltpu.roll(stored, 7, 1), pltpu.roll(stored, 1, 1))
        linear = (pulsation * swapped).reshape(points, spec_rows, block_size)
        out_ref[:, :, columns] = (
            coupled.reshape(points, spec_rows, block_size) + linear - source_ref[:, :, columns]
        )
        return carry

    def couple_part(part):
        count = block_count // COUPLING_COPIES
        load_coupling[part].wait()
        if part == 0:
            load_source.wait()
        lax.fori_loop(part * count, (part + 1) * count, couple, 0, unroll=count)

    back = []

    def nonlinear(c):
        for step in range(1, n_harm):
            there[c * (n_harm - 1) + step - 1].wait_recv()
        for i in range(c * piece, (c + 1) * piece):
            taken = jnp.concatenate(
                [columns_ref[:, i, p].reshape(rows, block_size) for p in range(points)], axis=1
            )
            voltage = jnp.dot(synthesis_ref[...], taken, preferred_element_type=jnp.float32)
            row = pl.ds(harm * share + i, 1)

            def wide(values):
                return jnp.concatenate([values] * points, axis=1)

            steep = wide(steepness_ref[row] * LOG2_E)
            scale = wide(saturation_ref[row] * LN_2)
            junction = wide(junction_ref[row])
            drive = steep * voltage
            current = scale * (
                jnp.maximum(drive, 0.0)
                + jnp.log(1.0 + jnp.exp2(-jnp.abs(drive))) * LOG2_E
                - 1.0
            )
            charge = junction * voltage * lax.rsqrt(1.0 + voltage * voltage)
            both = jnp.concatenate(
                [current.astype(jnp.bfloat16), charge.astype(jnp.bfloat16)], axis=0
            )
            combined = jnp.dot(analysis_ref[...], both, preferred_element_type=jnp.float32)
            combined = combined.astype(jnp.bfloat16)
            for p in range(points):
                back_ref[:, i, p] = combined[:, p * block_size : (p + 1) * block_size].reshape(
                    n_harm, spec_rows, block_size
                )
        for step in range(1, n_harm):
            peer = lax.rem(harm + step, n_harm)
            copy = pltpu.make_async_remote_copy(
                src_ref=back_ref.at[peer, pl.ds(c * piece, piece)],
                dst_ref=result_ref.at[harm, pl.ds(c * piece, piece)],
                send_sem=back_send_sem.at[c, step - 1],
                recv_sem=back_recv_sem.at[c, step - 1],
                device_id=(node, peer),
                device_id_type=MESH,
            )
            copy.start()
            back.append(copy)

    per_chunk = COUPLING_COPIES // CHUNKS
    for c in range(CHUNKS):
        nonlinear(c)
        for part in range(c * per_chunk, (c + 1) * per_chunk):
            couple_part(part)
    result_ref[harm] = back_ref[harm]

    for c in range(CHUNKS):
        for step in range(1, n_harm):
            back[c * (n_harm - 1) + step - 1].wait_recv()
        for q in range(n_harm):
            for i in range(c * piece, (c + 1) * piece):
                b = q * share + i
                span = pl.ds(b * block_size, block_size)
                out_ref[:, :, span] += result_ref[q, i].astype(jnp.float32)

    for copy in halo + there + back:
        copy.wait_send()


def solution(mesh):
    n_node, n_harm = mesh.shape["node"], mesh.shape["harm"]

    def local(
        spectrum,
        source,
        coupling,
        capacitance,
        saturation,
        steepness,
        junction,
        halo_list,
        neighbour_slot,
    ):
        spec_rows, points, node_count = spectrum.shape
        block_count, listed, block_size, _ = coupling.shape
        rows = spec_rows * n_harm
        share = block_count // n_harm
        slots = halo_list.shape[2]
        synthesis, analysis = tables(rows)
        halo_count = len(OFFSETS) * slots
        block = (points, spec_rows, block_size)
        vmem, smem = (pl.BlockSpec(memory_space=s) for s in (pltpu.VMEM, pltpu.SMEM))
        anywhere = pl.BlockSpec(memory_space=pl.ANY)
        dma = pltpu.SemaphoreType.DMA
        result = pl.pallas_call(
            functools.partial(body, n_node, n_harm),
            name="residual",
            out_shape=jax.ShapeDtypeStruct((points, spec_rows, node_count), jnp.float32),
            in_specs=[smem, smem, anywhere, anywhere, anywhere, vmem, vmem, vmem, vmem, vmem, vmem],
            out_specs=vmem,
            scratch_shapes=[
                pltpu.VMEM((points, spec_rows, node_count), jnp.float32),
                pltpu.VMEM((points, spec_rows, node_count), jnp.float32),
                pltpu.VMEM(coupling.shape, jnp.bfloat16),
                pltpu.VMEM((block_count + halo_count + 1, *block), jnp.bfloat16),
                pltpu.VMEM((halo_count, *block), jnp.bfloat16),
                pltpu.VMEM((halo_count, *block), jnp.bfloat16),
                pltpu.VMEM((n_harm, share, *block), jnp.bfloat16),
                pltpu.VMEM((n_harm, share, *block), jnp.bfloat16),
                pltpu.VMEM((n_harm, share, *block), jnp.bfloat16),
                dma((2 + COUPLING_COPIES,)),
                dma((len(OFFSETS),)),
                dma((len(OFFSETS),)),
                dma((CHUNKS, n_harm - 1)),
                dma((CHUNKS, n_harm - 1)),
                dma((CHUNKS, n_harm - 1)),
                dma((CHUNKS, n_harm - 1)),
            ],
            compiler_params=pltpu.CompilerParams(
                collective_id=0, has_side_effects=True, vmem_limit_bytes=40 * 2**20
            ),
        )(
            halo_list.transpose(1, 2, 0).reshape(halo_count, n_node),
            neighbour_slot.T,
            spectrum.transpose(1, 0, 2),
            source.transpose(1, 0, 2),
            coupling,
            capacitance.reshape(block_count, block_size),
            saturation.reshape(block_count, block_size),
            steepness.reshape(block_count, block_size),
            junction.reshape(block_count, block_size),
            jnp.asarray(synthesis, jnp.bfloat16),
            jnp.asarray(analysis, jnp.bfloat16),
        )
        return result.transpose(1, 0, 2)

    return jax.shard_map(
        local,
        mesh=mesh,
        in_specs=(
            P("harm", None, "node"),
            P("harm", None, "node"),
            P("node", None, None, None),
            P("node"),
            P("node"),
            P("node"),
            P("node"),
            P(),
            P("node", None),
        ),
        out_specs=P("harm", None, "node"),
        check_vma=False,
    )
```

time: 77 us -> 45.2 us (0.59)
  the two profiles are of different devices: /device:TPU:279 before, /device:TPU:1 now
where the time goes in v1:
time: 45.2 us; the launch traced here: 44.6 us
  Pallas kernels  32.3 us (71%)
  local copies, waits for them, and re-layouts  12.3 us (27%)
    pallas_call x1, Pallas kernels, local(): pl.pallas_call(functools.partial(body, n_node, n_harm), name='residual',...  32.3 us
    unnamed x23, local copies, waits for them, and re-layouts  12.3 us

profile of v1, /device:TPU:1, one launch (start us, length us, event | category | flops | bytes accessed | tf_op | source)
XLA Modules:
  0.0 44.6 jit_solution(5240007567943084530)
XLA Ops:
  0.0 0.0 copy-start
  0.0 2.8 %copy-done = bf16[48,4,128,128]{3,2,1,0:T(8,128)(2,1)S(1)} copy-done((bf16[48,4,128,128]{3,2,1,0:T(8,128)(2,1)S(1)}, bf16[48,4,128,128]{3,2,1,0:T(8,128)(2,1)}, u32[]{:S(2)}) %copy-start) | copy-done | bytes 6291480
  2.8 0.0 copy-start.1
  2.8 1.3 %copy-done.1 = f32[16,3,6144]{2,0,1:T(8,128)S(1)} copy-done((f32[16,3,6144]{2,0,1:T(8,128)S(1)}, f32[16,3,6144]{2,0,1:T(8,128)}, u32[]{:S(2)}) %copy-start.1) | copy-done | bytes 1179672
  4.1 0.0 copy-start.2
  4.1 1.3 %copy-done.2 = f32[16,3,6144]{2,0,1:T(8,128)S(1)} copy-done((f32[16,3,6144]{2,0,1:T(8,128)S(1)}, f32[16,3,6144]{2,0,1:T(8,128)}, u32[]{:S(2)}) %copy-start.2) | copy-done | bytes 1179672
  5.3 0.0 copy-start.3
  5.3 0.8 %copy-done.3 = bf16[128,256]{1,0:T(8,128)(2,1)S(1)} copy-done((bf16[128,256]{1,0:T(8,128)(2,1)S(1)}, bf16[128,256]{1,0:T(8,128)(2,1)}, u32[]{:S(2)}) %copy-start.3) | copy-done | bytes 65560
  6.2 0.0 copy-start.4
  6.2 0.8 %copy-done.4 = bf16[128,128]{1,0:T(8,128)(2,1)S(1)} copy-done((bf16[128,128]{1,0:T(8,128)(2,1)S(1)}, bf16[128,128]{1,0:T(8,128)(2,1)}, u32[]{:S(2)}) %copy-start.4) | copy-done | bytes 32792
  6.9 0.0 copy-start.5
  6.9 0.7 %copy-done.5 = f32[6144]{0:T(1024)S(1)} copy-done((f32[6144]{0:T(1024)S(1)}, f32[6144]{0:T(1024)}, u32[]{:S(2)}) %copy-start.5) | copy-done | bytes 24600
  7.7 0.0 copy-start.6
  7.7 0.7 %copy-done.6 = f32[6144]{0:T(1024)S(1)} copy-done((f32[6144]{0:T(1024)S(1)}, f32[6144]{0:T(1024)}, u32[]{:S(2)}) %copy-start.6) | copy-done | bytes 24600
  8.4 0.0 copy-start.7
  8.4 0.7 %copy-done.7 = f32[6144]{0:T(1024)S(1)} copy-done((f32[6144]{0:T(1024)S(1)}, f32[6144]{0:T(1024)}, u32[]{:S(2)}) %copy-start.7) | copy-done | bytes 24600
  9.1 0.0 copy-start.8
  9.1 0.7 %copy-done.8 = f32[6144]{0:T(1024)S(1)} copy-done((f32[6144]{0:T(1024)S(1)}, f32[6144]{0:T(1024)}, u32[]{:S(2)}) %copy-start.8) | copy-done | bytes 24600
  9.9 0.0 copy-start.9
  9.9 0.7 %copy-done.9 = s32[64,4,4]{0,2,1:T(4,128)S(1)} copy-done((s32[64,4,4]{0,2,1:T(4,128)S(1)}, s32[64,4,4]{0,2,1:T(4,128)}, u32[]{:S(2)}) %copy-start.9) | copy-done | bytes 4120
  10.6 0.0 copy-start.10
  10.6 0.7 %copy-done.10 = s32[48,4]{0,1:T(4,128)S(1)} copy-done((s32[48,4]{0,1:T(4,128)S(1)}, s32[48,4]{0,1:T(4,128)}, u32[]{:S(2)}) %copy-start.10) | copy-done | bytes 792
  11.3 32.3 %residual.1 = f32[3,16,6144]{2,1,0:T(8,128)S(1)} custom-call(s32[16,64]{1,0:T(8,128)S(1)} %bitcast.18, s32[4,48]{1,0:T(4,128)S(1)} %bitcast.19, f32[3,16,6144]{2,1,0:T(8,128)S(1)} %bitcast.12, f32[3,16,6144]{2,1,0:T(8,128)S(1)} %bitcast.13, bf16[48,4,128,128]{3,2,1,0:T(8,128)(2,1)S(1)} %copy-done, f32[48,128]{1,0:T(8,128)S(1)} %bitcast.14, ...), custom_call_target="tpu_custom_call" | custom-call | tf_op jit(solution)/shard_map/residual/pallas_call | solution.py:283
  43.5 1.0 %copy.13 = f32[16,3,6144]{2,0,1:T(8,128)} copy(f32[16,3,6144]{2,0,1:T(8,128)S(1)} %bitcast.11) | data formatting | bytes 2359296
Async XLA Ops:
  0.0 2.8 %copy-start = (bf16[48,4,128,128]{3,2,1,0:T(8,128)(2,1)S(1)}, bf16[48,4,128,128]{3,2,1,0:T(8,128)(2,1)}, u32[]{:S(2)}) copy-start(bf16[48,4,128,128]{3,2,1,0:T(8,128)(2,1)} %coupling_hbm.1) | copy-start | bytes 18874372
  2.8 1.3 %copy-start.1 = (f32[16,3,6144]{2,0,1:T(8,128)S(1)}, f32[16,3,6144]{2,0,1:T(8,128)}, u32[]{:S(2)}) copy-start(f32[16,3,6144]{2,0,1:T(8,128)} %param.11) | copy-start | bytes 3538948
  4.1 1.3 %copy-start.2 = (f32[16,3,6144]{2,0,1:T(8,128)S(1)}, f32[16,3,6144]{2,0,1:T(8,128)}, u32[]{:S(2)}) copy-start(f32[16,3,6144]{2,0,1:T(8,128)} %param.12) | copy-start | bytes 3538948
  5.3 0.8 %copy-start.3 = (bf16[128,256]{1,0:T(8,128)(2,1)S(1)}, bf16[128,256]{1,0:T(8,128)(2,1)}, u32[]{:S(2)}) copy-start(bf16[128,256]{1,0:T(8,128)(2,1)} %constant.5.clone.analysis_ref) | copy-start | bytes 196612
  6.2 0.8 %copy-start.4 = (bf16[128,128]{1,0:T(8,128)(2,1)S(1)}, bf16[128,128]{1,0:T(8,128)(2,1)}, u32[]{:S(2)}) copy-start(bf16[128,128]{1,0:T(8,128)(2,1)} %constant.4.clone.synthesis_ref) | copy-start | bytes 98308
  6.9 0.7 %copy-start.5 = (f32[6144]{0:T(1024)S(1)}, f32[6144]{0:T(1024)}, u32[]{:S(2)}) copy-start(f32[6144]{0:T(1024)} %param.14) | copy-start | bytes 73732
  7.7 0.7 %copy-start.6 = (f32[6144]{0:T(1024)S(1)}, f32[6144]{0:T(1024)}, u32[]{:S(2)}) copy-start(f32[6144]{0:T(1024)} %param.15) | copy-start | bytes 73732
  8.4 0.7 %copy-start.7 = (f32[6144]{0:T(1024)S(1)}, f32[6144]{0:T(1024)}, u32[]{:S(2)}) copy-start(f32[6144]{0:T(1024)} %param.16) | copy-start | bytes 73732
  9.1 0.7 %copy-start.8 = (f32[6144]{0:T(1024)S(1)}, f32[6144]{0:T(1024)}, u32[]{:S(2)}) copy-start(f32[6144]{0:T(1024)} %param.17) | copy-start | bytes 73732
  9.9 0.7 %copy-start.9 = (s32[64,4,4]{0,2,1:T(4,128)S(1)}, s32[64,4,4]{0,2,1:T(4,128)}, u32[]{:S(2)}) copy-start(s32[64,4,4]{0,2,1:T(4,128)} %param.18) | copy-start | bytes 12292
  10.6 0.7 %copy-start.10 = (s32[48,4]{0,1:T(4,128)S(1)}, s32[48,4]{0,1:T(4,128)}, u32[]{:S(2)}) copy-start(s32[48,4]{0,1:T(4,128)} %param.19) | copy-start | bytes 2308

commit v2 on v1

--- a/solution.py
+++ b/solution.py
@@ -72,15 +72,21 @@
     piece = share // CHUNKS
     rows = n_harm * spec_rows
     slots = halo_out_ref.shape[0] // len(OFFSETS)
-    neighbours = [lax.rem(node + offset + n_node, n_node) for offset in OFFSETS]
+    neighbours = [node + offset for offset in OFFSETS]
+    on_mesh = [(to >= 0) & (to < n_node) for to in neighbours]
+    greeted = sum(is_there.astype(jnp.int32) for is_there in on_mesh)
 
     barrier = pltpu.get_barrier_semaphore()
     for step in range(1, n_harm):
         pl.semaphore_signal(
             barrier, inc=1, device_id=(node, lax.rem(harm + step, n_harm)), device_id_type=MESH
         )
-    for neighbour in neighbours:
-        pl.semaphore_signal(barrier, inc=1, device_id=(neighbour, harm), device_id_type=MESH)
+    for neighbour, is_there in zip(neighbours, on_mesh):
+
+        @pl.when(is_there)
+        def _(neighbour=neighbour):
+            pl.semaphore_signal(barrier, inc=1, device_id=(neighbour, harm), device_id_type=MESH)
+
 
     load_spectrum = pltpu.make_async_copy(spectrum_hbm, spectrum_ref, load_sem.at[0])
     load_spectrum.start()
@@ -98,7 +104,8 @@
         copy.start()
     load_source.start()
 
-    load_spectrum.wait()
+    with jax.named_scope("spectrum_wait"):
+        load_spectrum.wait()
 
     def columns_of(b):
         return pl.ds(pl.multiple_of(b * block_size, block_size), block_size)
@@ -107,13 +114,15 @@
         blocks_ref[b] = spectrum_ref[:, :, columns_of(b)].astype(jnp.bfloat16)
         return carry
 
-    lax.fori_loop(0, block_count, round_block, 0, unroll=8)
+    with jax.named_scope("round"):
+        lax.fori_loop(0, block_count, round_block, 0, unroll=8)
     empty = block_count + len(OFFSETS) * slots
     blocks_ref[empty] = jnp.zeros(blocks_ref.shape[1:], jnp.bfloat16)
     for i in range(len(OFFSETS) * slots):
         halo_out_ref[i] = blocks_ref[halo_ref[i, node]]
 
-    pl.semaphore_wait(barrier, n_harm - 1 + len(OFFSETS))
+    with jax.named_scope("greeting"):
+        pl.semaphore_wait(barrier, n_harm - 1 + greeted)
 
     halo = []
     for j in range(len(OFFSETS)):
@@ -125,7 +134,7 @@
             device_id=(neighbours[j], harm),
             device_id_type=MESH,
         )
-        copy.start()
+        pl.when(on_mesh[j])(copy.start)
         halo.append(copy)
     there = []
     for c in range(CHUNKS):
@@ -143,8 +152,9 @@
             there.append(copy)
     columns_ref[harm] = blocks_ref[pl.ds(harm * share, share)]
 
-    for copy in halo:
-        copy.wait_recv()
+    with jax.named_scope("halo_wait"):
+        for j, copy in enumerate(halo):
+            pl.when(on_mesh[len(OFFSETS) - 1 - j])(copy.wait_recv)
     blocks_ref[pl.ds(block_count, len(OFFSETS) * slots)] = halo_in_ref[...]
 
     row_index = lax.broadcasted_iota(jnp.int32, (1, 8, block_size), 1)
@@ -186,13 +196,15 @@
         load_coupling[part].wait()
         if part == 0:
             load_source.wait()
-        lax.fori_loop(part * count, (part + 1) * count, couple, 0, unroll=count)
+        with jax.named_scope(f"couple_{part}"):
+            lax.fori_loop(part * count, (part + 1) * count, couple, 0, unroll=count)
 
     back = []
 
     def nonlinear(c):
-        for step in range(1, n_harm):
-            there[c * (n_harm - 1) + step - 1].wait_recv()
+        with jax.named_scope(f"there_wait_{c}"):
+            for step in range(1, n_harm):
+                there[c * (n_harm - 1) + step - 1].wait_recv()
         for i in range(c * piece, (c + 1) * piece):
             taken = jnp.concatenate(
                 [columns_ref[:, i, p].reshape(rows, block_size) for p in range(points)], axis=1
@@ -243,15 +255,18 @@
     result_ref[harm] = back_ref[harm]
 
     for c in range(CHUNKS):
-        for step in range(1, n_harm):
-            back[c * (n_harm - 1) + step - 1].wait_recv()
+        with jax.named_scope(f"back_wait_{c}"):
+            for step in range(1, n_harm):
+                back[c * (n_harm - 1) + step - 1].wait_recv()
         for q in range(n_harm):
             for i in range(c * piece, (c + 1) * piece):
                 b = q * share + i
                 span = pl.ds(b * block_size, block_size)
                 out_ref[:, :, span] += result_ref[q, i].astype(jnp.float32)
 
-    for copy in halo + there + back:
+    for is_there, copy in zip(on_mesh, halo):
+        pl.when(is_there)(copy.wait_send)
+    for copy in there + back:
         copy.wait_send()
 
 
@@ -305,7 +320,7 @@
                 dma((CHUNKS, n_harm - 1)),
             ],
             compiler_params=pltpu.CompilerParams(
-                collective_id=0, has_side_effects=True, vmem_limit_bytes=40 * 2**20
+                collective_id=0, has_side_effects=True, vmem_limit_bytes=62 * 2**20
             ),
         )(
             halo_list.transpose(1, 2, 0).reshape(halo_count, n_node),

time: 45.2 us -> 29.6 us (0.65)
  local copies, waits for them, and re-layouts: 12.3 us -> 2.36 us
  Pallas kernels: 32.3 us -> 27 us
    unnamed x23 -> x1, local copies, waits for them, and re-layouts: 12.3 us -> 2.36 us
    pallas_call x1, Pallas kernels: 32.3 us -> 27 us  [local(): pl.pallas_call(functools.partial(body, n_node, n_harm), name='residual',...]
where the time goes in v2:
time: 29.6 us; the launch traced here: 29.4 us
  Pallas kernels  27 us (91%)
  local copies, waits for them, and re-layouts  2.36 us (8%)
    pallas_call x1, Pallas kernels, local(): pl.pallas_call(functools.partial(body, n_node, n_harm), name='residual',...  27 us
    unnamed x1, local copies, waits for them, and re-layouts  2.36 us

profile of v2, /device:TPU:1, one launch (start us, length us, event | category | flops | bytes accessed | tf_op | source)
XLA Modules:
  0.0 29.4 jit_solution(13399795322258663489)
XLA Ops:
  0.0 27.0 %residual.1 = f32[3,16,6144]{2,1,0:T(8,128)} custom-call(s32[16,64]{1,0:T(8,128)} %bitcast.18, s32[4,48]{1,0:T(4,128)} %bitcast.19, f32[3,16,6144]{2,1,0:T(8,128)} %bitcast.12, f32[3,16,6144]{2,1,0:T(8,128)} %bitcast.13, bf16[48,4,128,128]{3,2,1,0:T(8,128)(2,1)} %coupling_hbm.1, f32[48,128]{1,0:T(8,128)} %bitcast.14, f32[48,128]{1,0:T(8,128)} %bitcast.15, ...), custom_call_target="tpu_custom_call" | custom-call | tf_op jit(solution)/shard_map/residual/pallas_call | solution.py:298
  27.0 2.4 %copy.13 = f32[16,3,6144]{2,0,1:T(8,128)} copy(f32[16,3,6144]{2,0,1:T(8,128)} %bitcast.11) | data formatting | bytes 2359296

commit v3 on v2

--- a/solution.py
+++ b/solution.py
@@ -35,18 +35,26 @@
 def body(
     n_node,
     n_harm,
-    halo_ref,
-    slot_ref,
+    halo_hbm,
+    slot_hbm,
     spectrum_hbm,
     source_hbm,
     coupling_hbm,
+    capacitance_hbm,
+    saturation_hbm,
+    steepness_hbm,
+    junction_hbm,
+    synthesis_hbm,
+    analysis_hbm,
+    out_ref,
+    halo_ref,
+    slot_ref,
     capacitance_ref,
     saturation_ref,
     steepness_ref,
     junction_ref,
     synthesis_ref,
     analysis_ref,
-    out_ref,
     spectrum_ref,
     source_ref,
     coupling_ref,
@@ -56,6 +64,7 @@
     columns_ref,
     back_ref,
     result_ref,
+    small_sem,
     load_sem,
     halo_send_sem,
     halo_recv_sem,
@@ -76,6 +85,8 @@
     on_mesh = [(to >= 0) & (to < n_node) for to in neighbours]
     greeted = sum(is_there.astype(jnp.int32) for is_there in on_mesh)
 
+    load_spectrum = pltpu.make_async_copy(spectrum_hbm, spectrum_ref, load_sem.at[0])
+    load_spectrum.start()
     barrier = pltpu.get_barrier_semaphore()
     for step in range(1, n_harm):
         pl.semaphore_signal(
@@ -88,21 +99,33 @@
             pl.semaphore_signal(barrier, inc=1, device_id=(neighbour, harm), device_id_type=MESH)
 
 
-    load_spectrum = pltpu.make_async_copy(spectrum_hbm, spectrum_ref, load_sem.at[0])
-    load_spectrum.start()
-    load_source = pltpu.make_async_copy(source_hbm, source_ref, load_sem.at[1])
+    whole = [
+        (halo_hbm, halo_ref),
+        (synthesis_hbm, synthesis_ref),
+        (analysis_hbm, analysis_ref),
+        (saturation_hbm, saturation_ref),
+        (steepness_hbm, steepness_ref),
+        (junction_hbm, junction_ref),
+        (slot_hbm, slot_ref),
+        (capacitance_hbm, capacitance_ref),
+        (source_hbm, source_ref),
+    ]
+    loads = [
+        pltpu.make_async_copy(source, target, small_sem.at[i])
+        for i, (source, target) in enumerate(whole)
+    ]
     per_copy = block_count // COUPLING_COPIES
     load_coupling = [
         pltpu.make_async_copy(
             coupling_hbm.at[pl.ds(i * per_copy, per_copy)],
             coupling_ref.at[pl.ds(i * per_copy, per_copy)],
-            load_sem.at[2 + i],
+            load_sem.at[1 + i],
         )
         for i in range(COUPLING_COPIES)
     ]
-    for copy in load_coupling:
+    load_halo, for_nonlinear, for_linear = loads[0], loads[1:6], loads[6:]
+    for copy in loads + load_coupling:
         copy.start()
-    load_source.start()
 
     with jax.named_scope("spectrum_wait"):
         load_spectrum.wait()
@@ -118,6 +141,7 @@
         lax.fori_loop(0, block_count, round_block, 0, unroll=8)
     empty = block_count + len(OFFSETS) * slots
     blocks_ref[empty] = jnp.zeros(blocks_ref.shape[1:], jnp.bfloat16)
+    load_halo.wait()
     for i in range(len(OFFSETS) * slots):
         halo_out_ref[i] = blocks_ref[halo_ref[i, node]]
 
@@ -151,11 +175,16 @@
             copy.start()
             there.append(copy)
     columns_ref[harm] = blocks_ref[pl.ds(harm * share, share)]
-
-    with jax.named_scope("halo_wait"):
-        for j, copy in enumerate(halo):
-            pl.when(on_mesh[len(OFFSETS) - 1 - j])(copy.wait_recv)
-    blocks_ref[pl.ds(block_count, len(OFFSETS) * slots)] = halo_in_ref[...]
+    for copy in for_nonlinear:
+        copy.wait()
+
+    def take_halo():
+        with jax.named_scope("halo_wait"):
+            for j, copy in enumerate(halo):
+                pl.when(on_mesh[len(OFFSETS) - 1 - j])(copy.wait_recv)
+        blocks_ref[pl.ds(block_count, len(OFFSETS) * slots)] = halo_in_ref[...]
+        for copy in for_linear:
+            copy.wait()
 
     row_index = lax.broadcasted_iota(jnp.int32, (1, 8, block_size), 1)
     even = row_index % 2 == 0
@@ -194,8 +223,6 @@
     def couple_part(part):
         count = block_count // COUPLING_COPIES
         load_coupling[part].wait()
-        if part == 0:
-            load_source.wait()
         with jax.named_scope(f"couple_{part}"):
             lax.fori_loop(part * count, (part + 1) * count, couple, 0, unroll=count)
 
@@ -247,11 +274,16 @@
             copy.start()
             back.append(copy)
 
-    per_chunk = COUPLING_COPIES // CHUNKS
     for c in range(CHUNKS):
         nonlinear(c)
-        for part in range(c * per_chunk, (c + 1) * per_chunk):
-            couple_part(part)
+        if c == CHUNKS - 2:
+            take_halo()
+        if c == CHUNKS - 2:
+            couple_part(0)
+            couple_part(1)
+        if c == CHUNKS - 1:
+            for part in range(2, COUPLING_COPIES):
+                couple_part(part)
     result_ref[harm] = back_ref[harm]
 
     for c in range(CHUNKS):
@@ -292,16 +324,20 @@
         synthesis, analysis = tables(rows)
         halo_count = len(OFFSETS) * slots
         block = (points, spec_rows, block_size)
-        vmem, smem = (pl.BlockSpec(memory_space=s) for s in (pltpu.VMEM, pltpu.SMEM))
-        anywhere = pl.BlockSpec(memory_space=pl.ANY)
+        held = functools.partial(pltpu.with_memory_space_constraint, memory_space=pltpu.HBM)
         dma = pltpu.SemaphoreType.DMA
         result = pl.pallas_call(
             functools.partial(body, n_node, n_harm),
             name="residual",
-            out_shape=jax.ShapeDtypeStruct((points, spec_rows, node_count), jnp.float32),
-            in_specs=[smem, smem, anywhere, anywhere, anywhere, vmem, vmem, vmem, vmem, vmem, vmem],
-            out_specs=vmem,
+            out_shape=pltpu.VMEM((points, spec_rows, node_count), jnp.float32),
+            in_specs=[pl.BlockSpec(memory_space=pltpu.HBM)] * 11,
+            out_specs=pl.BlockSpec(memory_space=pltpu.VMEM),
             scratch_shapes=[
+                pltpu.SMEM((halo_count, n_node), jnp.int32),
+                pltpu.SMEM((listed, block_count), jnp.int32),
+                *[pltpu.VMEM((block_count, block_size), jnp.float32)] * 4,
+                pltpu.VMEM((rows, rows), jnp.bfloat16),
+                pltpu.VMEM((rows, 2 * rows), jnp.bfloat16),
                 pltpu.VMEM((points, spec_rows, node_count), jnp.float32),
                 pltpu.VMEM((points, spec_rows, node_count), jnp.float32),
                 pltpu.VMEM(coupling.shape, jnp.bfloat16),
@@ -311,7 +347,8 @@
                 pltpu.VMEM((n_harm, share, *block), jnp.bfloat16),
                 pltpu.VMEM((n_harm, share, *block), jnp.bfloat16),
                 pltpu.VMEM((n_harm, share, *block), jnp.bfloat16),
-                dma((2 + COUPLING_COPIES,)),
+                dma((9,)),
+                dma((1 + COUPLING_COPIES,)),
                 dma((len(OFFSETS),)),
                 dma((len(OFFSETS),)),
                 dma((CHUNKS, n_harm - 1)),
@@ -320,20 +357,20 @@
                 dma((CHUNKS, n_harm - 1)),
             ],
             compiler_params=pltpu.CompilerParams(
-                collective_id=0, has_side_effects=True, vmem_limit_bytes=62 * 2**20
+                collective_id=0, has_side_effects=True, vmem_limit_bytes=40 * 2**20
             ),
         )(
-            halo_list.transpose(1, 2, 0).reshape(halo_count, n_node),
-            neighbour_slot.T,
-            spectrum.transpose(1, 0, 2),
-            source.transpose(1, 0, 2),
-            coupling,
-            capacitance.reshape(block_count, block_size),
-            saturation.reshape(block_count, block_size),
-            steepness.reshape(block_count, block_size),
-            junction.reshape(block_count, block_size),
-            jnp.asarray(synthesis, jnp.bfloat16),
-            jnp.asarray(analysis, jnp.bfloat16),
+            held(halo_list.transpose(1, 2, 0).reshape(halo_count, n_node)),
+            held(neighbour_slot.T),
+            held(spectrum.transpose(1, 0, 2)),
+            held(source.transpose(1, 0, 2)),
+            held(coupling),
+            held(capacitance.reshape(block_count, block_size)),
+            held(saturation.reshape(block_count, block_size)),
+            held(steepness.reshape(block_count, block_size)),
+            held(junction.reshape(block_count, block_size)),
+            held(jnp.asarray(synthesis, jnp.bfloat16)),
+            held(jnp.asarray(analysis, jnp.bfloat16)),
         )
         return result.transpose(1, 0, 2)
 

time: 29.6 us -> 26.3 us (0.89)
  Pallas kernels: 27 us -> 25.1 us
  local copies, waits for them, and re-layouts: 2.36 us -> 1.02 us
    pallas_call x1, Pallas kernels: 27 us -> 25.1 us  [local(): pl.pallas_call(functools.partial(body, n_node, n_harm), name='residual',...]
    unnamed x1, local copies, waits for them, and re-layouts: 2.36 us -> 1.02 us
where the time goes in v3:
time: 26.3 us; the launch traced here: 26.1 us
  Pallas kernels  25.1 us (95%)
  local copies, waits for them, and re-layouts  1.02 us (4%)
    pallas_call x1, Pallas kernels, local(): pl.pallas_call(functools.partial(body, n_node, n_harm), name='residual',...  25.1 us
    unnamed x1, local copies, waits for them, and re-layouts  1.02 us

profile of v3, /device:TPU:1, one launch (start us, length us, event | category | flops | bytes accessed | tf_op | source)
XLA Modules:
  0.0 26.1 jit_solution(1191457820103105821)
XLA Ops:
  0.0 25.1 %residual.1 = f32[3,16,6144]{2,1,0:T(8,128)S(1)} custom-call(s32[16,64]{1,0:T(8,128)} %bitcast.18, s32[4,48]{1,0:T(4,128)} %bitcast.19, f32[3,16,6144]{2,1,0:T(8,128)} %bitcast.12, f32[3,16,6144]{2,1,0:T(8,128)} %bitcast.13, bf16[48,4,128,128]{3,2,1,0:T(8,128)(2,1)} %coupling_hbm.1, f32[48,128]{1,0:T(8,128)} %bitcast.14, f32[48,128]{1,0:T(8,128)} %bitcast.15, ...), custom_call_target="tpu_custom_call" | custom-call | tf_op jit(solution)/shard_map/residual/pallas_call | solution.py:329
  25.1 1.0 %copy.13 = f32[16,3,6144]{2,0,1:T(8,128)} copy(f32[16,3,6144]{2,0,1:T(8,128)S(1)} %bitcast.11) | data formatting | bytes 2359296

commit v4 on v3

v4 whole, which is shorter than its diff:
```python
import functools

import jax
import jax.numpy as jnp
import numpy as np
from jax import lax
from jax.experimental import pallas as pl
from jax.experimental.pallas import tpu as pltpu
from jax.sharding import PartitionSpec as P

OFFSETS = (-2, -1, 1, 2)
LOG2_E = 1.4426950408889634
LN_2 = 0.6931471805599453
MESH = pl.DeviceIdType.MESH
CHUNKS = 3
COUPLING_COPIES = 6
Y_SIZE = 8


def tables(rows):
    time = np.arange(rows)[:, None]
    row = np.arange(rows)[None, :]
    phase = (row // 2) * time % rows
    angle = 2.0 * np.pi / rows * phase
    synthesis = np.where(row % 2 == 1, np.sin(angle), np.cos(angle))
    synthesis = np.where(row == 1, np.where(time % 2 == 0, 1.0, -1.0), synthesis)
    weights = np.where(np.arange(rows) < 2, 1.0 / rows, 2.0 / rows)
    analysis = synthesis.T * weights[:, None]
    pulsation = (np.arange(rows) // 2)[:, None] / (rows // 2)
    derived = np.empty_like(analysis)
    derived[0::2] = pulsation[0::2] * analysis[1::2]
    derived[1::2] = -pulsation[1::2] * analysis[0::2]
    return synthesis, np.concatenate([analysis, derived], axis=1)


def body(
    n_node,
    n_harm,
    halo_hbm,
    slot_hbm,
    spectrum_hbm,
    source_hbm,
    coupling_hbm,
    capacitance_hbm,
    saturation_hbm,
    steepness_hbm,
    junction_hbm,
    synthesis_hbm,
    analysis_hbm,
    out_ref,
    halo_ref,
    slot_ref,
    capacitance_ref,
    saturation_ref,
    steepness_ref,
    junction_ref,
    synthesis_ref,
    analysis_ref,
    spectrum_ref,
    source_ref,
    coupling_ref,
    blocks_ref,
    halo_out_ref,
    halo_in_ref,
    columns_ref,
    back_ref,
    result_ref,
    small_sem,
    spectrum_sem,
    coupling_sem,
    halo_send_sem,
    halo_recv_sem,
    there_send_sem,
    there_recv_sem,
    back_send_sem,
    back_recv_sem,
    node_sem,
    late_sem,
):
    node = lax.axis_index("node")
    harm = lax.axis_index("harm")
    points, spec_rows, _ = spectrum_ref.shape
    block_count, listed, block_size, _ = coupling_ref.shape
    span = block_count // CHUNKS
    piece = span // n_harm
    rows = n_harm * spec_rows
    slots = halo_out_ref.shape[0] // len(OFFSETS)
    peers = [lax.rem(harm + step, n_harm) for step in range(1, n_harm)]
    neighbours = [node + offset for offset in OFFSETS]

    last = (node == 0) & (harm == 0)
    with_last = (node == 0) & (harm > 0)

    def nearness(place):
        off = 2 * lax.rem(place, Y_SIZE) - Y_SIZE - 1
        return off * off

    later, earlier = [], []
    for to, offset in zip(neighbours, OFFSETS):
        on_mesh = (to >= 0) & (to < n_node)
        to_near, own_near = nearness(to), nearness(node)
        follows = to_near < own_near
        if offset > 0:
            follows = follows | (to_near == own_near)
        follows = ((to == 0) & (harm == 0)) | (follows & ~last)
        later.append(on_mesh & follows)
        earlier.append(on_mesh & ~follows)

    def count(flags):
        return sum(flag.astype(jnp.int32) for flag in flags)

    barrier = pltpu.get_barrier_semaphore()

    @pl.when(~last)
    def _():
        for peer in peers:
            pl.semaphore_signal(barrier, inc=1, device_id=(node, peer), device_id_type=MESH)

    for neighbour, flag in zip(neighbours, later):

        @pl.when(flag)
        def _(neighbour=neighbour):
            pl.semaphore_signal(barrier, inc=1, device_id=(neighbour, harm), device_id_type=MESH)

    width = span * block_size
    load_spectrum = [
        pltpu.make_async_copy(
            spectrum_hbm.at[:, :, pl.ds(c * width, width)],
            spectrum_ref.at[:, :, pl.ds(c * width, width)],
            spectrum_sem.at[c],
        )
        for c in range(CHUNKS)
    ]
    for copy in load_spectrum:
        copy.start()
    whole = [
        (halo_hbm, halo_ref),
        (synthesis_hbm, synthesis_ref),
        (analysis_hbm, analysis_ref),
        (saturation_hbm, saturation_ref),
        (steepness_hbm, steepness_ref),
        (junction_hbm, junction_ref),
        (slot_hbm, slot_ref),
        (capacitance_hbm, capacitance_ref),
        (source_hbm, source_ref),
    ]
    loads = [
        pltpu.make_async_copy(source, target, small_sem.at[i])
        for i, (source, target) in enumerate(whole)
    ]
    load_halo, for_nonlinear, for_linear = loads[0], loads[1:6], loads[6:]
    load_halo.start()
    for copy in for_nonlinear:
        copy.start()
    per_copy = block_count // COUPLING_COPIES
    load_coupling = [
        pltpu.make_async_copy(
            coupling_hbm.at[pl.ds(i * per_copy, per_copy)],
            coupling_ref.at[pl.ds(i * per_copy, per_copy)],
            coupling_sem.at[i],
        )
        for i in range(COUPLING_COPIES)
    ]

    def columns_of(b):
        return pl.ds(pl.multiple_of(b * block_size, block_size), block_size)

    def round_block(b, carry):
        blocks_ref[b] = spectrum_ref[:, :, columns_of(b)].astype(jnp.bfloat16)
        return carry

    there_chunks = [
        [
            pltpu.make_async_remote_copy(
                src_ref=blocks_ref.at[pl.ds(c * span + peer * piece, piece)],
                dst_ref=columns_ref.at[pl.ds(c * span + harm * piece, piece)],
                send_sem=there_send_sem,
                recv_sem=there_recv_sem.at[c],
                device_id=(node, peer),
                device_id_type=MESH,
            )
            for peer in peers
        ]
        for c in range(CHUNKS)
    ]
    for c in range(CHUNKS):
        with jax.named_scope(f"spectrum_wait_{c}"):
            load_spectrum[c].wait()
        lax.fori_loop(c * span, (c + 1) * span, round_block, 0, unroll=8)
        if c == 0:
            with jax.named_scope("greeting"):
                pl.semaphore_wait(
                    barrier, n_harm - 1 - with_last.astype(jnp.int32) + count(earlier)
                )

            @pl.when(last)
            def _():
                for peer in peers:
                    pl.semaphore_signal(
                        late_sem, inc=1, device_id=(node, peer), device_id_type=MESH
                    )

        for peer, copy in zip(peers, there_chunks[c]):
            pl.when(~(with_last & (peer == 0)))(copy.start)
    for neighbour, flag in zip(neighbours, earlier):

        @pl.when(flag)
        def _(neighbour=neighbour):
            pl.semaphore_signal(node_sem, inc=1, device_id=(neighbour, harm), device_id_type=MESH)

    load_halo.wait()
    for i in range(len(OFFSETS) * slots):
        halo_out_ref[i] = blocks_ref[halo_ref[i, node]]
    empty = block_count + len(OFFSETS) * slots
    blocks_ref[empty] = jnp.zeros(blocks_ref.shape[1:], jnp.bfloat16)
    halo = [
        pltpu.make_async_remote_copy(
            src_ref=halo_out_ref.at[pl.ds(j * slots, slots)],
            dst_ref=halo_in_ref.at[pl.ds(j * slots, slots)],
            send_sem=halo_send_sem.at[j],
            recv_sem=halo_recv_sem.at[j],
            device_id=(neighbour, harm),
            device_id_type=MESH,
        )
        for j, neighbour in enumerate(neighbours)
    ]
    for copy, flag in zip(halo, earlier):
        pl.when(flag)(copy.start)
    for copy in for_linear + load_coupling:
        copy.start()
    for c in range(CHUNKS):
        at = pl.ds(c * span + harm * piece, piece)
        columns_ref[at] = blocks_ref[at]
    for copy in for_nonlinear:
        copy.wait()

    @pl.when(with_last)
    def _():
        with jax.named_scope("last_wait"):
            pl.semaphore_wait(late_sem, 1)
        for chunk in there_chunks:
            for peer, copy in zip(peers, chunk):
                pl.when(peer == 0)(copy.start)

    def bytes_of(buffer, blocks, sem):
        part = buffer.at[pl.ds(0, blocks)]
        return pltpu.make_async_copy(part, part, sem)

    back = []

    def nonlinear(c):
        with jax.named_scope(f"there_wait_{c}"):
            bytes_of(columns_ref, (n_harm - 1) * piece, there_recv_sem.at[c]).wait()
        for i in range(piece):
            taken = jnp.concatenate(
                [
                    jnp.concatenate(
                        [columns_ref[c * span + q * piece + i, p] for q in range(n_harm)], axis=0
                    )
                    for p in range(points)
                ],
                axis=1,
            )
            voltage = jnp.dot(synthesis_ref[...], taken, preferred_element_type=jnp.float32)
            row = pl.ds(c * span + harm * piece + i, 1)

            def wide(values):
                return jnp.concatenate([values] * points, axis=1)

            steep = wide(steepness_ref[row] * LOG2_E)
            scale = wide(saturation_ref[row] * LN_2)
            junction = wide(junction_ref[row])
            drive = steep * voltage
            current = scale * (
                jnp.maximum(drive, 0.0)
                + jnp.log(1.0 + jnp.exp2(-jnp.abs(drive))) * LOG2_E
                - 1.0
            )
            charge = junction * voltage * lax.rsqrt(1.0 + voltage * voltage)
            both = jnp.concatenate(
                [current.astype(jnp.bfloat16), charge.astype(jnp.bfloat16)], axis=0
            )
            combined = jnp.dot(analysis_ref[...], both, preferred_element_type=jnp.float32)
            combined = combined.astype(jnp.bfloat16)
            for q in range(n_harm):
                for p in range(points):
                    back_ref[c * span + q * piece + i, p] = combined[
                        q * spec_rows : (q + 1) * spec_rows,
                        p * block_size : (p + 1) * block_size,
                    ]
        for peer in peers:
            copy = pltpu.make_async_remote_copy(
                src_ref=back_ref.at[pl.ds(c * span + peer * piece, piece)],
                dst_ref=result_ref.at[pl.ds(c * span + harm * piece, piece)],
                send_sem=back_send_sem,
                recv_sem=back_recv_sem.at[c],
                device_id=(node, peer),
                device_id_type=MESH,
            )
            copy.start()
            back.append(copy)

    row_index = lax.broadcasted_iota(jnp.int32, (1, 8, block_size), 1)
    even = row_index % 2 == 0
    tiles = spec_rows // 8
    pulsations = []
    for i in range(tiles):
        harmonic = (harm * spec_rows + i * 8 + row_index) // 2
        value = harmonic.astype(jnp.float32) * (2.0 / rows)
        pulsations.append(jnp.where(even, value, -value))
    pulsation = jnp.concatenate(pulsations * points, axis=0)

    def couple(b, carry):
        gathered = jnp.concatenate(
            [
                blocks_ref[slot_ref[k, b]].reshape(points * spec_rows, block_size)
                for k in range(listed)
            ],
            axis=1,
        )
        matrix = jnp.concatenate([coupling_ref[b, k] for k in range(listed)], axis=1)
        coupled = lax.dot_general(
            gathered, matrix, (((1,), (1,)), ((), ())), preferred_element_type=jnp.float32
        )
        columns = columns_of(b)
        stored = capacitance_ref[pl.ds(b, 1)] * spectrum_ref[:, :, columns].reshape(
            points * spec_rows, block_size
        )
        stored = stored.reshape(points * tiles, 8, block_size)
        swapped = jnp.where(even, pltpu.roll(stored, 7, 1), pltpu.roll(stored, 1, 1))
        linear = (pulsation * swapped).reshape(points, spec_rows, block_size)
        out_ref[:, :, columns] = (
            coupled.reshape(points, spec_rows, block_size) + linear - source_ref[:, :, columns]
        )
        return carry

    nonlinear(0)
    with jax.named_scope("node_wait"):
        awaited = count(later)

        @pl.when(awaited > 0)
        def _():
            pl.semaphore_wait(node_sem, awaited)

    for copy, flag in zip(halo, later):
        pl.when(flag)(copy.start)
    for c in range(1, CHUNKS):
        nonlinear(c)
    for c in range(CHUNKS):
        at = pl.ds(c * span + harm * piece, piece)
        result_ref[at] = back_ref[at]
    with jax.named_scope("halo_wait"):
        for j, copy in enumerate(halo):
            opposite = len(OFFSETS) - 1 - j
            pl.when(later[opposite] | earlier[opposite])(copy.wait_recv)
    blocks_ref[pl.ds(block_count, len(OFFSETS) * slots)] = halo_in_ref[...]
    for copy in for_linear:
        copy.wait()
    for part in range(COUPLING_COPIES):
        load_coupling[part].wait()
        with jax.named_scope(f"couple_{part}"):
            lax.fori_loop(part * per_copy, (part + 1) * per_copy, couple, 0, unroll=per_copy)

    for c in range(CHUNKS):
        with jax.named_scope(f"back_wait_{c}"):
            bytes_of(result_ref, (n_harm - 1) * piece, back_recv_sem.at[c]).wait()
        if c == CHUNKS - 1:
            with jax.named_scope("sent"):
                for copy, up, down in zip(halo, later, earlier):
                    pl.when(up | down)(copy.wait_send)
                sent = CHUNKS * (n_harm - 1) * piece
                bytes_of(blocks_ref, sent, there_send_sem).wait()
                bytes_of(back_ref, sent, back_send_sem).wait()
        with jax.named_scope(f"add_{c}"):
            for b in range(c * span, (c + 1) * span):
                at = pl.ds(b * block_size, block_size)
                out_ref[:, :, at] += result_ref[b].astype(jnp.float32)


def solution(mesh):
    n_node, n_harm = mesh.shape["node"], mesh.shape["harm"]

    def local(
        spectrum,
        source,
        coupling,
        capacitance,
        saturation,
        steepness,
        junction,
        halo_list,
        neighbour_slot,
    ):
        spec_rows, points, node_count = spectrum.shape
        block_count, listed, block_size, _ = coupling.shape
        rows = spec_rows * n_harm
        slots = halo_list.shape[2]
        synthesis, analysis = tables(rows)
        halo_count = len(OFFSETS) * slots
        block = (points, spec_rows, block_size)
        held = functools.partial(pltpu.with_memory_space_constraint, memory_space=pltpu.HBM)
        dma = pltpu.SemaphoreType.DMA
        result = pl.pallas_call(
            functools.partial(body, n_node, n_harm),
            name="residual",
            out_shape=pltpu.VMEM((points, spec_rows, node_count), jnp.float32),
            in_specs=[pl.BlockSpec(memory_space=pltpu.HBM)] * 11,
            out_specs=pl.BlockSpec(memory_space=pltpu.VMEM),
            scratch_shapes=[
                pltpu.SMEM((halo_count, n_node), jnp.int32),
                pltpu.SMEM((listed, block_count), jnp.int32),
                *[pltpu.VMEM((block_count, block_size), jnp.float32)] * 4,
                pltpu.VMEM((rows, rows), jnp.bfloat16),
                pltpu.VMEM((rows, 2 * rows), jnp.bfloat16),
                pltpu.VMEM((points, spec_rows, node_count), jnp.float32),
                pltpu.VMEM((points, spec_rows, node_count), jnp.float32),
                pltpu.VMEM(coupling.shape, jnp.bfloat16),
                pltpu.VMEM((block_count + halo_count + 1, *block), jnp.bfloat16),
                pltpu.VMEM((halo_count, *block), jnp.bfloat16),
                pltpu.VMEM((halo_count, *block), jnp.bfloat16),
                *[pltpu.VMEM((block_count, *block), jnp.bfloat16)] * 3,
                dma((9,)),
                dma((CHUNKS,)),
                dma((COUPLING_COPIES,)),
                dma((len(OFFSETS),)),
                dma((len(OFFSETS),)),
                dma,
                dma((CHUNKS,)),
                dma,
                dma((CHUNKS,)),
                pltpu.SemaphoreType.REGULAR,
                pltpu.SemaphoreType.REGULAR,
            ],
            compiler_params=pltpu.CompilerParams(
                collective_id=0, has_side_effects=True, vmem_limit_bytes=40 * 2**20
            ),
        )(
            held(halo_list.transpose(1, 2, 0).reshape(halo_count, n_node)),
            held(neighbour_slot.T),
            held(spectrum.transpose(1, 0, 2)),
            held(source.transpose(1, 0, 2)),
            held(coupling),
            held(capacitance.reshape(block_count, block_size)),
            held(saturation.reshape(block_count, block_size)),
            held(steepness.reshape(block_count, block_size)),
            held(junction.reshape(block_count, block_size)),
            held(jnp.asarray(synthesis, jnp.bfloat16)),
            held(jnp.asarray(analysis, jnp.bfloat16)),
        )
        return result.transpose(1, 0, 2)

    return jax.shard_map(
        local,
        mesh=mesh,
        in_specs=(
            P("harm", None, "node"),
            P("harm", None, "node"),
            P("node", None, None, None),
            P("node"),
            P("node"),
            P("node"),
            P("node"),
            P(),
            P("node", None),
        ),
        out_specs=P("harm", None, "node"),
        check_vma=False,
    )
```

time: 26.3 us -> 23.6 us (0.90)
  Pallas kernels: 25.1 us -> 22.4 us
    pallas_call x1, Pallas kernels: 25.1 us -> 22.4 us  [local(): pl.pallas_call(functools.partial(body, n_node, n_harm), name='residual',...]
where the time goes in v4:
time: 23.6 us; the launch traced here: 23.4 us
  Pallas kernels  22.4 us (95%)
  local copies, waits for them, and re-layouts  1.02 us (4%)
    pallas_call x1, Pallas kernels, local(): pl.pallas_call(functools.partial(body, n_node, n_harm), name='residual',...  22.4 us
    unnamed x1, local copies, waits for them, and re-layouts  1.02 us

profile of v4, /device:TPU:1, one launch (start us, length us, event | category | flops | bytes accessed | tf_op | source)
XLA Modules:
  0.0 23.4 jit_solution(2931760379346502720)
XLA Ops:
  0.0 22.4 %residual.1 = f32[3,16,6144]{2,1,0:T(8,128)S(1)} custom-call(s32[16,64]{1,0:T(8,128)} %bitcast.18, s32[4,48]{1,0:T(4,128)} %bitcast.19, f32[3,16,6144]{2,1,0:T(8,128)} %bitcast.12, f32[3,16,6144]{2,1,0:T(8,128)} %bitcast.13, bf16[48,4,128,128]{3,2,1,0:T(8,128)(2,1)} %coupling_hbm.1, f32[48,128]{1,0:T(8,128)} %bitcast.14, f32[48,128]{1,0:T(8,128)} %bitcast.15, ...), custom_call_target="tpu_custom_call" | custom-call | tf_op jit(solution)/shard_map/residual/pallas_call | solution.py:403
  22.4 1.0 %copy.13 = f32[16,3,6144]{2,0,1:T(8,128)} copy(f32[16,3,6144]{2,0,1:T(8,128)S(1)} %bitcast.11) | data formatting | bytes 2359296

commit v5 on v4

--- a/solution.py
+++ b/solution.py
@@ -14,6 +14,7 @@
 MESH = pl.DeviceIdType.MESH
 CHUNKS = 3
 COUPLING_COPIES = 6
+EARLY_PARTS = 3
 Y_SIZE = 8
 
 
@@ -76,6 +77,9 @@
     back_recv_sem,
     node_sem,
     late_sem,
+    proxy_ref,
+    proxy_back_ref,
+    proxy_sem,
 ):
     node = lax.axis_index("node")
     harm = lax.axis_index("harm")
@@ -85,42 +89,40 @@
     piece = span // n_harm
     rows = n_harm * spec_rows
     slots = halo_out_ref.shape[0] // len(OFFSETS)
-    peers = [lax.rem(harm + step, n_harm) for step in range(1, n_harm)]
+    chips = n_harm // 2
+    turns = [(0, 1)] + [(ahead, core) for core in (0, 1) for ahead in (2, 3, 1)]
+    peers = [
+        lax.rem(harm // 2 + ahead, chips) * 2 + lax.rem(harm + core, 2) for ahead, core in turns
+    ]
     neighbours = [node + offset for offset in OFFSETS]
 
     last = (node == 0) & (harm == 0)
     with_last = (node == 0) & (harm > 0)
-
-    def nearness(place):
-        off = 2 * lax.rem(place, Y_SIZE) - Y_SIZE - 1
-        return off * off
+    proxy = (node == 0) & (harm == 1)
+
+    middle = n_node // Y_SIZE // 2
+
+    def upper_follows(lower, distance):
+        y, above = lax.rem(lower, Y_SIZE), lower // Y_SIZE + 1
+        low_off = 2 * y - Y_SIZE - 1
+        high_off = 2 * lax.rem(y + distance, Y_SIZE) - Y_SIZE - 1
+        crosses = y + distance >= Y_SIZE
+        across = above == middle
+        if distance == 2:
+            across = across | ((above < middle) & (y == Y_SIZE - 1))
+        along = high_off * high_off <= low_off * low_off
+        return (crosses & across) | (~crosses & along)
 
     later, earlier = [], []
     for to, offset in zip(neighbours, OFFSETS):
         on_mesh = (to >= 0) & (to < n_node)
-        to_near, own_near = nearness(to), nearness(node)
-        follows = to_near < own_near
-        if offset > 0:
-            follows = follows | (to_near == own_near)
+        follows = upper_follows(node, offset) if offset > 0 else ~upper_follows(to, -offset)
         follows = ((to == 0) & (harm == 0)) | (follows & ~last)
         later.append(on_mesh & follows)
         earlier.append(on_mesh & ~follows)
 
     def count(flags):
         return sum(flag.astype(jnp.int32) for flag in flags)
-
-    barrier = pltpu.get_barrier_semaphore()
-
-    @pl.when(~last)
-    def _():
-        for peer in peers:
-            pl.semaphore_signal(barrier, inc=1, device_id=(node, peer), device_id_type=MESH)
-
-    for neighbour, flag in zip(neighbours, later):
-
-        @pl.when(flag)
-        def _(neighbour=neighbour):
-            pl.semaphore_signal(barrier, inc=1, device_id=(neighbour, harm), device_id_type=MESH)
 
     width = span * block_size
     load_spectrum = [
@@ -133,6 +135,19 @@
     ]
     for copy in load_spectrum:
         copy.start()
+    barrier = pltpu.get_barrier_semaphore()
+
+    @pl.when(~last)
+    def _():
+        for peer in peers:
+            pl.semaphore_signal(barrier, inc=1, device_id=(node, peer), device_id_type=MESH)
+
+    for neighbour, flag in zip(neighbours, later):
+
+        @pl.when(flag)
+        def _(neighbour=neighbour):
+            pl.semaphore_signal(barrier, inc=1, device_id=(neighbour, harm), device_id_type=MESH)
+
     whole = [
         (halo_hbm, halo_ref),
         (synthesis_hbm, synthesis_ref),
@@ -202,6 +217,18 @@
 
         for peer, copy in zip(peers, there_chunks[c]):
             pl.when(~(with_last & (peer == 0)))(copy.start)
+
+        @pl.when((node == 0) & ~proxy)
+        def _(c=c):
+            pltpu.make_async_remote_copy(
+                src_ref=blocks_ref.at[pl.ds(c * span, piece)],
+                dst_ref=proxy_ref.at[pl.ds(c * span + harm * piece, piece)],
+                send_sem=there_send_sem,
+                recv_sem=proxy_sem.at[c],
+                device_id=(node, 1),
+                device_id_type=MESH,
+            ).start()
+
     for neighbour, flag in zip(neighbours, earlier):
 
         @pl.when(flag)
@@ -231,74 +258,93 @@
     for c in range(CHUNKS):
         at = pl.ds(c * span + harm * piece, piece)
         columns_ref[at] = blocks_ref[at]
+
+    @pl.when(proxy)
+    def _():
+        for c in range(CHUNKS):
+            proxy_ref[pl.ds(c * span + piece, piece)] = blocks_ref[pl.ds(c * span, piece)]
+
     for copy in for_nonlinear:
         copy.wait()
-
-    @pl.when(with_last)
-    def _():
-        with jax.named_scope("last_wait"):
-            pl.semaphore_wait(late_sem, 1)
-        for chunk in there_chunks:
-            for peer, copy in zip(peers, chunk):
-                pl.when(peer == 0)(copy.start)
 
     def bytes_of(buffer, blocks, sem):
         part = buffer.at[pl.ds(0, blocks)]
         return pltpu.make_async_copy(part, part, sem)
 
-    back = []
-
-    def nonlinear(c):
-        with jax.named_scope(f"there_wait_{c}"):
-            bytes_of(columns_ref, (n_harm - 1) * piece, there_recv_sem.at[c]).wait()
-        for i in range(piece):
-            taken = jnp.concatenate(
-                [
-                    jnp.concatenate(
-                        [columns_ref[c * span + q * piece + i, p] for q in range(n_harm)], axis=0
-                    )
-                    for p in range(points)
-                ],
-                axis=1,
-            )
-            voltage = jnp.dot(synthesis_ref[...], taken, preferred_element_type=jnp.float32)
-            row = pl.ds(c * span + harm * piece + i, 1)
-
-            def wide(values):
-                return jnp.concatenate([values] * points, axis=1)
-
-            steep = wide(steepness_ref[row] * LOG2_E)
-            scale = wide(saturation_ref[row] * LN_2)
-            junction = wide(junction_ref[row])
-            drive = steep * voltage
-            current = scale * (
-                jnp.maximum(drive, 0.0)
-                + jnp.log(1.0 + jnp.exp2(-jnp.abs(drive))) * LOG2_E
-                - 1.0
-            )
-            charge = junction * voltage * lax.rsqrt(1.0 + voltage * voltage)
-            both = jnp.concatenate(
-                [current.astype(jnp.bfloat16), charge.astype(jnp.bfloat16)], axis=0
-            )
-            combined = jnp.dot(analysis_ref[...], both, preferred_element_type=jnp.float32)
-            combined = combined.astype(jnp.bfloat16)
-            for q in range(n_harm):
-                for p in range(points):
-                    back_ref[c * span + q * piece + i, p] = combined[
+    def evaluate(row, read, write):
+        taken = jnp.concatenate(
+            [jnp.concatenate([read(q, p) for q in range(n_harm)], axis=0) for p in range(points)],
+            axis=1,
+        )
+        voltage = jnp.dot(synthesis_ref[...], taken, preferred_element_type=jnp.float32)
+
+        def wide(values):
+            return jnp.concatenate([values] * points, axis=1)
+
+        steep = wide(steepness_ref[row] * LOG2_E)
+        scale = wide(saturation_ref[row] * LN_2)
+        junction = wide(junction_ref[row])
+        drive = steep * voltage
+        current = scale * (
+            jnp.maximum(drive, 0.0) + jnp.log(1.0 + jnp.exp2(-jnp.abs(drive))) * LOG2_E - 1.0
+        )
+        charge = junction * voltage * lax.rsqrt(1.0 + voltage * voltage)
+        both = jnp.concatenate([current.astype(jnp.bfloat16), charge.astype(jnp.bfloat16)], axis=0)
+        combined = jnp.dot(analysis_ref[...], both, preferred_element_type=jnp.float32)
+        combined = combined.astype(jnp.bfloat16)
+        for q in range(n_harm):
+            for p in range(points):
+                write(
+                    q,
+                    p,
+                    combined[
                         q * spec_rows : (q + 1) * spec_rows,
                         p * block_size : (p + 1) * block_size,
-                    ]
+                    ],
+                )
+
+    def evaluate_chunk(c, owner, taken_ref, given_ref, send_sem):
+        for i in range(piece):
+
+            def read(q, p):
+                return taken_ref[c * span + q * piece + i, p]
+
+            def write(q, p, values):
+                given_ref[c * span + q * piece + i, p] = values
+
+            evaluate(pl.ds(c * span + owner * piece + i, 1), read, write)
         for peer in peers:
-            copy = pltpu.make_async_remote_copy(
-                src_ref=back_ref.at[pl.ds(c * span + peer * piece, piece)],
-                dst_ref=result_ref.at[pl.ds(c * span + harm * piece, piece)],
-                send_sem=back_send_sem,
+            pltpu.make_async_remote_copy(
+                src_ref=given_ref.at[pl.ds(c * span + peer * piece, piece)],
+                dst_ref=result_ref.at[pl.ds(c * span + owner * piece, piece)],
+                send_sem=send_sem,
                 recv_sem=back_recv_sem.at[c],
                 device_id=(node, peer),
                 device_id_type=MESH,
-            )
-            copy.start()
-            back.append(copy)
+            ).start()
+        result_ref[pl.ds(c * span + owner * piece, piece)] = given_ref[
+            pl.ds(c * span + harm * piece, piece)
+        ]
+
+    whole_share = (n_harm - 1) * piece
+
+    def nonlinear(c):
+        with jax.named_scope(f"there_wait_{c}"):
+            bytes_of(columns_ref, whole_share, there_recv_sem.at[c]).wait()
+        if c == 0:
+
+            @pl.when(with_last)
+            def _():
+                with jax.named_scope("last_wait"):
+                    pl.semaphore_wait(late_sem, 1)
+
+        evaluate_chunk(c, harm, columns_ref, back_ref, back_send_sem)
+
+        @pl.when(proxy)
+        def _():
+            with jax.named_scope(f"proxy_wait_{c}"):
+                bytes_of(proxy_ref, whole_share, proxy_sem.at[c]).wait()
+            evaluate_chunk(c, 0, proxy_ref, proxy_back_ref, proxy_sem.at[CHUNKS])
 
     row_index = lax.broadcasted_iota(jnp.int32, (1, 8, block_size), 1)
     even = row_index % 2 == 0
@@ -334,7 +380,6 @@
         )
         return carry
 
-    nonlinear(0)
     with jax.named_scope("node_wait"):
         awaited = count(later)
 
@@ -344,33 +389,62 @@
 
     for copy, flag in zip(halo, later):
         pl.when(flag)(copy.start)
-    for c in range(1, CHUNKS):
-        nonlinear(c)
-    for c in range(CHUNKS):
-        at = pl.ds(c * span + harm * piece, piece)
-        result_ref[at] = back_ref[at]
-    with jax.named_scope("halo_wait"):
-        for j, copy in enumerate(halo):
-            opposite = len(OFFSETS) - 1 - j
-            pl.when(later[opposite] | earlier[opposite])(copy.wait_recv)
-    blocks_ref[pl.ds(block_count, len(OFFSETS) * slots)] = halo_in_ref[...]
-    for copy in for_linear:
-        copy.wait()
-    for part in range(COUPLING_COPIES):
-        load_coupling[part].wait()
-        with jax.named_scope(f"couple_{part}"):
-            lax.fori_loop(part * per_copy, (part + 1) * per_copy, couple, 0, unroll=per_copy)
-
+
+    def take_halo():
+        with jax.named_scope("halo_wait"):
+            for j, copy in enumerate(halo):
+                opposite = len(OFFSETS) - 1 - j
+                pl.when(later[opposite] | earlier[opposite])(copy.wait_recv)
+        blocks_ref[pl.ds(block_count, len(OFFSETS) * slots)] = halo_in_ref[...]
+        for copy in for_linear:
+            copy.wait()
+
+    def couple_part(part, carry):
+        first = part * per_copy
+        pltpu.make_async_copy(
+            coupling_hbm.at[pl.ds(first, per_copy)],
+            coupling_ref.at[pl.ds(first, per_copy)],
+            coupling_sem.at[part],
+        ).wait()
+        for i in range(per_copy):
+            couple(first + i, 0)
+        return carry
+
+    early = jnp.where(proxy, EARLY_PARTS, 0)
+
+    @pl.when(proxy)
+    def _():
+        take_halo()
+        with jax.named_scope("couple_early"):
+            lax.fori_loop(0, EARLY_PARTS, couple_part, 0)
+
+    @pl.when(~last)
+    def _():
+        for c in range(CHUNKS):
+            nonlinear(c)
+
+    pl.when(~proxy)(take_halo)
+    with jax.named_scope("couple"):
+        lax.fori_loop(early, COUPLING_COPIES, couple_part, 0)
+
+    def wait_blocks(flag, buffer, blocks, sem):
+        pl.when(flag)(lambda: bytes_of(buffer, blocks, sem).wait())
+
+    plain = ~last & ~proxy
     for c in range(CHUNKS):
         with jax.named_scope(f"back_wait_{c}"):
-            bytes_of(result_ref, (n_harm - 1) * piece, back_recv_sem.at[c]).wait()
+            wait_blocks(plain, result_ref, whole_share, back_recv_sem.at[c])
+            wait_blocks(proxy, result_ref, whole_share - piece, back_recv_sem.at[c])
+            wait_blocks(last, result_ref, whole_share + piece, back_recv_sem.at[c])
         if c == CHUNKS - 1:
             with jax.named_scope("sent"):
                 for copy, up, down in zip(halo, later, earlier):
                     pl.when(up | down)(copy.wait_send)
-                sent = CHUNKS * (n_harm - 1) * piece
-                bytes_of(blocks_ref, sent, there_send_sem).wait()
-                bytes_of(back_ref, sent, back_send_sem).wait()
+                wait_blocks(plain, blocks_ref, CHUNKS * whole_share, there_send_sem)
+                wait_blocks(proxy, blocks_ref, CHUNKS * (whole_share - piece), there_send_sem)
+                wait_blocks(last, blocks_ref, CHUNKS * (whole_share + piece), there_send_sem)
+                wait_blocks(~last, back_ref, CHUNKS * whole_share, back_send_sem)
+                wait_blocks(proxy, back_ref, CHUNKS * whole_share, proxy_sem.at[CHUNKS])
         with jax.named_scope(f"add_{c}"):
             for b in range(c * span, (c + 1) * span):
                 at = pl.ds(b * block_size, block_size)
@@ -430,6 +504,9 @@
                 dma((CHUNKS,)),
                 pltpu.SemaphoreType.REGULAR,
                 pltpu.SemaphoreType.REGULAR,
+                pltpu.VMEM((block_count, *block), jnp.bfloat16),
+                pltpu.VMEM((block_count, *block), jnp.bfloat16),
+                dma((CHUNKS + 1,)),
             ],
             compiler_params=pltpu.CompilerParams(
                 collective_id=0, has_side_effects=True, vmem_limit_bytes=40 * 2**20

time: 23.6 us -> 22.9 us (0.970)
  Pallas kernels: 22.4 us -> 21.7 us
    pallas_call x1, Pallas kernels: 22.4 us -> 21.7 us  [local(): pl.pallas_call(functools.partial(body, n_node, n_harm), name='residual',...]
where the time goes in v5:
time: 22.9 us; the launch traced here: 22.7 us
  Pallas kernels  21.7 us (95%)
  local copies, waits for them, and re-layouts  1.02 us (4%)
    pallas_call x1, Pallas kernels, local(): pl.pallas_call(functools.partial(body, n_node, n_harm), name='residual',...  21.7 us
    unnamed x1, local copies, waits for them, and re-layouts  1.02 us

profile of v5, /device:TPU:1, one launch (start us, length us, event | category | flops | bytes accessed | tf_op | source)
XLA Modules:
  0.0 22.7 jit_solution(18139895055908259488)
XLA Ops:
  0.0 21.7 %residual.1 = f32[3,16,6144]{2,1,0:T(8,128)S(1)} custom-call(s32[16,64]{1,0:T(8,128)} %bitcast.18, s32[4,48]{1,0:T(4,128)} %bitcast.19, f32[3,16,6144]{2,1,0:T(8,128)} %bitcast.12, f32[3,16,6144]{2,1,0:T(8,128)} %bitcast.13, bf16[48,4,128,128]{3,2,1,0:T(8,128)(2,1)} %coupling_hbm.1, f32[48,128]{1,0:T(8,128)} %bitcast.14, f32[48,128]{1,0:T(8,128)} %bitcast.15, ...), custom_call_target="tpu_custom_call" | custom-call | tf_op jit(solution)/shard_map/residual/pallas_call | solution.py:477
  21.7 1.0 %copy.13 = f32[16,3,6144]{2,0,1:T(8,128)} copy(f32[16,3,6144]{2,0,1:T(8,128)S(1)} %bitcast.11) | data formatting | bytes 2359296

commit v6 on v5

--- a/solution.py
+++ b/solution.py
@@ -12,7 +12,8 @@
 LOG2_E = 1.4426950408889634
 LN_2 = 0.6931471805599453
 MESH = pl.DeviceIdType.MESH
-CHUNKS = 3
+PIECES = (1, 1, 2, 2)
+CHUNKS = len(PIECES)
 COUPLING_COPIES = 6
 EARLY_PARTS = 3
 Y_SIZE = 8
@@ -85,8 +86,12 @@
     harm = lax.axis_index("harm")
     points, spec_rows, _ = spectrum_ref.shape
     block_count, listed, block_size, _ = coupling_ref.shape
-    span = block_count // CHUNKS
-    piece = span // n_harm
+    share = block_count // n_harm
+    starts = [n_harm * sum(PIECES[:c]) for c in range(CHUNKS + 1)]
+
+    def blocks_of(c, owner):
+        return pl.ds(starts[c] + owner * PIECES[c], PIECES[c])
+
     rows = n_harm * spec_rows
     slots = halo_out_ref.shape[0] // len(OFFSETS)
     chips = n_harm // 2
@@ -109,7 +114,7 @@
         crosses = y + distance >= Y_SIZE
         across = above == middle
         if distance == 2:
-            across = across | ((above < middle) & (y == Y_SIZE - 1))
+            across = (above <= middle) & (y == Y_SIZE - 1)
         along = high_off * high_off <= low_off * low_off
         return (crosses & across) | (~crosses & along)
 
@@ -124,15 +129,14 @@
     def count(flags):
         return sum(flag.astype(jnp.int32) for flag in flags)
 
-    width = span * block_size
-    load_spectrum = [
-        pltpu.make_async_copy(
-            spectrum_hbm.at[:, :, pl.ds(c * width, width)],
-            spectrum_ref.at[:, :, pl.ds(c * width, width)],
-            spectrum_sem.at[c],
-        )
-        for c in range(CHUNKS)
-    ]
+    load_spectrum = []
+    for c in range(CHUNKS):
+        at = pl.ds(starts[c] * block_size, (starts[c + 1] - starts[c]) * block_size)
+        load_spectrum.append(
+            pltpu.make_async_copy(
+                spectrum_hbm.at[:, :, at], spectrum_ref.at[:, :, at], spectrum_sem.at[c]
+            )
+        )
     for copy in load_spectrum:
         copy.start()
     barrier = pltpu.get_barrier_semaphore()
@@ -187,8 +191,8 @@
     there_chunks = [
         [
             pltpu.make_async_remote_copy(
-                src_ref=blocks_ref.at[pl.ds(c * span + peer * piece, piece)],
-                dst_ref=columns_ref.at[pl.ds(c * span + harm * piece, piece)],
+                src_ref=blocks_ref.at[blocks_of(c, peer)],
+                dst_ref=columns_ref.at[blocks_of(c, harm)],
                 send_sem=there_send_sem,
                 recv_sem=there_recv_sem.at[c],
                 device_id=(node, peer),
@@ -201,33 +205,31 @@
     for c in range(CHUNKS):
         with jax.named_scope(f"spectrum_wait_{c}"):
             load_spectrum[c].wait()
-        lax.fori_loop(c * span, (c + 1) * span, round_block, 0, unroll=8)
+        lax.fori_loop(starts[c], starts[c + 1], round_block, 0, unroll=8)
         if c == 0:
             with jax.named_scope("greeting"):
                 pl.semaphore_wait(
                     barrier, n_harm - 1 - with_last.astype(jnp.int32) + count(earlier)
                 )
 
-            @pl.when(last)
-            def _():
-                for peer in peers:
-                    pl.semaphore_signal(
-                        late_sem, inc=1, device_id=(node, peer), device_id_type=MESH
-                    )
-
         for peer, copy in zip(peers, there_chunks[c]):
             pl.when(~(with_last & (peer == 0)))(copy.start)
 
         @pl.when((node == 0) & ~proxy)
         def _(c=c):
             pltpu.make_async_remote_copy(
-                src_ref=blocks_ref.at[pl.ds(c * span, piece)],
-                dst_ref=proxy_ref.at[pl.ds(c * span + harm * piece, piece)],
+                src_ref=blocks_ref.at[blocks_of(c, 0)],
+                dst_ref=proxy_ref.at[blocks_of(c, harm)],
                 send_sem=there_send_sem,
                 recv_sem=proxy_sem.at[c],
                 device_id=(node, 1),
                 device_id_type=MESH,
             ).start()
+
+    @pl.when(last)
+    def _():
+        for peer in peers:
+            pl.semaphore_signal(late_sem, inc=1, device_id=(node, peer), device_id_type=MESH)
 
     for neighbour, flag in zip(neighbours, earlier):
 
@@ -256,13 +258,12 @@
     for copy in for_linear + load_coupling:
         copy.start()
     for c in range(CHUNKS):
-        at = pl.ds(c * span + harm * piece, piece)
-        columns_ref[at] = blocks_ref[at]
+        columns_ref[blocks_of(c, harm)] = blocks_ref[blocks_of(c, harm)]
 
     @pl.when(proxy)
     def _():
         for c in range(CHUNKS):
-            proxy_ref[pl.ds(c * span + piece, piece)] = blocks_ref[pl.ds(c * span, piece)]
+            proxy_ref[blocks_of(c, 1)] = blocks_ref[blocks_of(c, 0)]
 
     for copy in for_nonlinear:
         copy.wait()
@@ -303,34 +304,40 @@
                     ],
                 )
 
+    def give(c, owner, given_ref, peer, send_sem):
+        return pltpu.make_async_remote_copy(
+            src_ref=given_ref.at[blocks_of(c, peer)],
+            dst_ref=result_ref.at[blocks_of(c, owner)],
+            send_sem=send_sem,
+            recv_sem=back_recv_sem.at[c],
+            device_id=(node, peer),
+            device_id_type=MESH,
+        )
+
+    deferring = (node == 0) & (harm > 1)
+
     def evaluate_chunk(c, owner, taken_ref, given_ref, send_sem):
-        for i in range(piece):
+        for i in range(PIECES[c]):
 
             def read(q, p):
-                return taken_ref[c * span + q * piece + i, p]
+                return taken_ref[starts[c] + q * PIECES[c] + i, p]
 
             def write(q, p, values):
-                given_ref[c * span + q * piece + i, p] = values
-
-            evaluate(pl.ds(c * span + owner * piece + i, 1), read, write)
-        for peer in peers:
-            pltpu.make_async_remote_copy(
-                src_ref=given_ref.at[pl.ds(c * span + peer * piece, piece)],
-                dst_ref=result_ref.at[pl.ds(c * span + owner * piece, piece)],
-                send_sem=send_sem,
-                recv_sem=back_recv_sem.at[c],
-                device_id=(node, peer),
-                device_id_type=MESH,
-            ).start()
-        result_ref[pl.ds(c * span + owner * piece, piece)] = given_ref[
-            pl.ds(c * span + harm * piece, piece)
-        ]
-
-    whole_share = (n_harm - 1) * piece
+                given_ref[starts[c] + q * PIECES[c] + i, p] = values
+
+            evaluate(pl.ds(starts[c] + owner * PIECES[c] + i, 1), read, write)
+        order = [(peer, ~(deferring & (peer == 0))) for peer in peers]
+        if c == CHUNKS - 1:
+            order = [(1, harm != 1), (0, (harm != 0) & ~deferring)] + [
+                (peer, peer > 1) for peer in peers
+            ]
+        for peer, flag in order:
+            pl.when(flag)(give(c, owner, given_ref, peer, send_sem).start)
+        result_ref[blocks_of(c, owner)] = given_ref[blocks_of(c, harm)]
 
     def nonlinear(c):
         with jax.named_scope(f"there_wait_{c}"):
-            bytes_of(columns_ref, whole_share, there_recv_sem.at[c]).wait()
+            bytes_of(columns_ref, (n_harm - 1) * PIECES[c], there_recv_sem.at[c]).wait()
         if c == 0:
 
             @pl.when(with_last)
@@ -343,7 +350,7 @@
         @pl.when(proxy)
         def _():
             with jax.named_scope(f"proxy_wait_{c}"):
-                bytes_of(proxy_ref, whole_share, proxy_sem.at[c]).wait()
+                bytes_of(proxy_ref, (n_harm - 1) * PIECES[c], proxy_sem.at[c]).wait()
             evaluate_chunk(c, 0, proxy_ref, proxy_back_ref, proxy_sem.at[CHUNKS])
 
     row_index = lax.broadcasted_iota(jnp.int32, (1, 8, block_size), 1)
@@ -423,6 +430,11 @@
         for c in range(CHUNKS):
             nonlinear(c)
 
+        @pl.when(deferring)
+        def _():
+            for c in range(CHUNKS):
+                give(c, harm, back_ref, 0, back_send_sem).start()
+
     pl.when(~proxy)(take_halo)
     with jax.named_scope("couple"):
         lax.fori_loop(early, COUPLING_COPIES, couple_part, 0)
@@ -433,20 +445,20 @@
     plain = ~last & ~proxy
     for c in range(CHUNKS):
         with jax.named_scope(f"back_wait_{c}"):
-            wait_blocks(plain, result_ref, whole_share, back_recv_sem.at[c])
-            wait_blocks(proxy, result_ref, whole_share - piece, back_recv_sem.at[c])
-            wait_blocks(last, result_ref, whole_share + piece, back_recv_sem.at[c])
+            wait_blocks(plain, result_ref, (n_harm - 1) * PIECES[c], back_recv_sem.at[c])
+            wait_blocks(proxy, result_ref, (n_harm - 2) * PIECES[c], back_recv_sem.at[c])
+            wait_blocks(last, result_ref, n_harm * PIECES[c], back_recv_sem.at[c])
         if c == CHUNKS - 1:
             with jax.named_scope("sent"):
                 for copy, up, down in zip(halo, later, earlier):
                     pl.when(up | down)(copy.wait_send)
-                wait_blocks(plain, blocks_ref, CHUNKS * whole_share, there_send_sem)
-                wait_blocks(proxy, blocks_ref, CHUNKS * (whole_share - piece), there_send_sem)
-                wait_blocks(last, blocks_ref, CHUNKS * (whole_share + piece), there_send_sem)
-                wait_blocks(~last, back_ref, CHUNKS * whole_share, back_send_sem)
-                wait_blocks(proxy, back_ref, CHUNKS * whole_share, proxy_sem.at[CHUNKS])
+                wait_blocks(plain, blocks_ref, (n_harm - 1) * share, there_send_sem)
+                wait_blocks(proxy, blocks_ref, (n_harm - 2) * share, there_send_sem)
+                wait_blocks(last, blocks_ref, n_harm * share, there_send_sem)
+                wait_blocks(~last, back_ref, (n_harm - 1) * share, back_send_sem)
+                wait_blocks(proxy, back_ref, (n_harm - 1) * share, proxy_sem.at[CHUNKS])
         with jax.named_scope(f"add_{c}"):
-            for b in range(c * span, (c + 1) * span):
+            for b in range(starts[c], starts[c + 1]):
                 at = pl.ds(b * block_size, block_size)
                 out_ref[:, :, at] += result_ref[b].astype(jnp.float32)
 

time: 22.9 us -> 21.1 us (0.921)
  the two profiles are of different devices: /device:TPU:1 before, /device:TPU:240 now
where the time goes in v6:
time: 21.1 us; the launch traced here: 21 us
  Pallas kernels  20 us (95%)
  local copies, waits for them, and re-layouts  1.02 us (5%)
    pallas_call x1, Pallas kernels, local(): pl.pallas_call(functools.partial(body, n_node, n_harm), name='residual',...  20 us
    unnamed x1, local copies, waits for them, and re-layouts  1.02 us

profile of v6, /device:TPU:240, one launch (start us, length us, event | category | flops | bytes accessed | tf_op | source)
XLA Modules:
  0.0 21.0 jit_solution(7275993832175542540)
XLA Ops:
  0.0 20.0 %residual.1 = f32[3,16,6144]{2,1,0:T(8,128)S(1)} custom-call(s32[16,64]{1,0:T(8,128)} %bitcast.18, s32[4,48]{1,0:T(4,128)} %bitcast.19, f32[3,16,6144]{2,1,0:T(8,128)} %bitcast.12, f32[3,16,6144]{2,1,0:T(8,128)} %bitcast.13, bf16[48,4,128,128]{3,2,1,0:T(8,128)(2,1)} %coupling_hbm.1, f32[48,128]{1,0:T(8,128)} %bitcast.14, f32[48,128]{1,0:T(8,128)} %bitcast.15, ...), custom_call_target="tpu_custom_call" | custom-call | tf_op jit(solution)/shard_map/residual/pallas_call | solution.py:489
  20.0 1.0 %copy.13 = f32[16,3,6144]{2,0,1:T(8,128)} copy(f32[16,3,6144]{2,0,1:T(8,128)S(1)} %bitcast.11) | data formatting | bytes 2359296

commit v7 on v6

--- a/solution.py
+++ b/solution.py
@@ -106,15 +106,17 @@
     proxy = (node == 0) & (harm == 1)
 
     middle = n_node // Y_SIZE // 2
+    halves = lax.rem(harm // 2, 2) == 1
 
     def upper_follows(lower, distance):
         y, above = lax.rem(lower, Y_SIZE), lower // Y_SIZE + 1
         low_off = 2 * y - Y_SIZE - 1
         high_off = 2 * lax.rem(y + distance, Y_SIZE) - Y_SIZE - 1
         crosses = y + distance >= Y_SIZE
-        across = above == middle
+        across = (above == middle) & halves
         if distance == 2:
-            across = (above <= middle) & (y == Y_SIZE - 1)
+            far = y == Y_SIZE - 1
+            across = across | ((above < middle) & far & halves) | ((above == middle) & far)
         along = high_off * high_off <= low_off * low_off
         return (crosses & across) | (~crosses & along)
 

time: 21.1 us -> 20.9 us (level)
  Pallas kernels: 20 us -> 19.7 us
    pallas_call x1, Pallas kernels: 20 us -> 19.7 us  [local(): pl.pallas_call(functools.partial(body, n_node, n_harm), name='residual',...]
where the time goes in v7:
time: 20.9 us; the launch traced here: 20.7 us
  Pallas kernels  19.7 us (94%)
  local copies, waits for them, and re-layouts  1.02 us (5%)
    pallas_call x1, Pallas kernels, local(): pl.pallas_call(functools.partial(body, n_node, n_harm), name='residual',...  19.7 us
    unnamed x1, local copies, waits for them, and re-layouts  1.02 us

profile of v7, /device:TPU:240, one launch (start us, length us, event | category | flops | bytes accessed | tf_op | source)
XLA Modules:
  0.0 20.7 jit_solution(6246374741492623406)
XLA Ops:
  0.0 19.7 %residual.1 = f32[3,16,6144]{2,1,0:T(8,128)S(1)} custom-call(s32[16,64]{1,0:T(8,128)} %bitcast.18, s32[4,48]{1,0:T(4,128)} %bitcast.19, f32[3,16,6144]{2,1,0:T(8,128)} %bitcast.12, f32[3,16,6144]{2,1,0:T(8,128)} %bitcast.13, bf16[48,4,128,128]{3,2,1,0:T(8,128)(2,1)} %coupling_hbm.1, f32[48,128]{1,0:T(8,128)} %bitcast.14, f32[48,128]{1,0:T(8,128)} %bitcast.15, ...), custom_call_target="tpu_custom_call" | custom-call | tf_op jit(solution)/shard_map/residual/pallas_call | solution.py:491
  19.7 1.0 %copy.13 = f32[16,3,6144]{2,0,1:T(8,128)} copy(f32[16,3,6144]{2,0,1:T(8,128)S(1)} %bitcast.11) | data formatting | bytes 2359296

commit v8 on v7

--- a/solution.py
+++ b/solution.py
@@ -14,7 +14,7 @@
 MESH = pl.DeviceIdType.MESH
 PIECES = (1, 1, 2, 2)
 CHUNKS = len(PIECES)
-COUPLING_COPIES = 6
+COUPLING_PARTS = 6
 EARLY_PARTS = 3
 Y_SIZE = 8
 
@@ -173,15 +173,8 @@
     load_halo.start()
     for copy in for_nonlinear:
         copy.start()
-    per_copy = block_count // COUPLING_COPIES
-    load_coupling = [
-        pltpu.make_async_copy(
-            coupling_hbm.at[pl.ds(i * per_copy, per_copy)],
-            coupling_ref.at[pl.ds(i * per_copy, per_copy)],
-            coupling_sem.at[i],
-        )
-        for i in range(COUPLING_COPIES)
-    ]
+    per_part = block_count // COUPLING_PARTS
+    load_coupling = pltpu.make_async_copy(coupling_hbm, coupling_ref, coupling_sem)
 
     def columns_of(b):
         return pl.ds(pl.multiple_of(b * block_size, block_size), block_size)
@@ -257,7 +250,7 @@
     ]
     for copy, flag in zip(halo, earlier):
         pl.when(flag)(copy.start)
-    for copy in for_linear + load_coupling:
+    for copy in [*for_linear, load_coupling]:
         copy.start()
     for c in range(CHUNKS):
         columns_ref[blocks_of(c, harm)] = blocks_ref[blocks_of(c, harm)]
@@ -329,7 +322,7 @@
 
             evaluate(pl.ds(starts[c] + owner * PIECES[c] + i, 1), read, write)
         order = [(peer, ~(deferring & (peer == 0))) for peer in peers]
-        if c == CHUNKS - 1:
+        if c >= CHUNKS - 2:
             order = [(1, harm != 1), (0, (harm != 0) & ~deferring)] + [
                 (peer, peer > 1) for peer in peers
             ]
@@ -405,17 +398,12 @@
                 opposite = len(OFFSETS) - 1 - j
                 pl.when(later[opposite] | earlier[opposite])(copy.wait_recv)
         blocks_ref[pl.ds(block_count, len(OFFSETS) * slots)] = halo_in_ref[...]
-        for copy in for_linear:
+        for copy in [*for_linear, load_coupling]:
             copy.wait()
 
     def couple_part(part, carry):
-        first = part * per_copy
-        pltpu.make_async_copy(
-            coupling_hbm.at[pl.ds(first, per_copy)],
-            coupling_ref.at[pl.ds(first, per_copy)],
-            coupling_sem.at[part],
-        ).wait()
-        for i in range(per_copy):
+        first = part * per_part
+        for i in range(per_part):
             couple(first + i, 0)
         return carry
 
@@ -439,7 +427,7 @@
 
     pl.when(~proxy)(take_halo)
     with jax.named_scope("couple"):
-        lax.fori_loop(early, COUPLING_COPIES, couple_part, 0)
+        lax.fori_loop(early, COUPLING_PARTS, couple_part, 0)
 
     def wait_blocks(flag, buffer, blocks, sem):
         pl.when(flag)(lambda: bytes_of(buffer, blocks, sem).wait())
@@ -509,7 +497,7 @@
                 *[pltpu.VMEM((block_count, *block), jnp.bfloat16)] * 3,
                 dma((9,)),
                 dma((CHUNKS,)),
-                dma((COUPLING_COPIES,)),
+                dma,
                 dma((len(OFFSETS),)),
                 dma((len(OFFSETS),)),
                 dma,

time: 20.9 us -> 20.8 us (level)
  no operation moved by 1% of the time
where the time goes in v8:
time: 20.8 us; the launch traced here: 20.7 us
  Pallas kernels  19.7 us (95%)
  local copies, waits for them, and re-layouts  1.02 us (5%)
    pallas_call x1, Pallas kernels, local(): pl.pallas_call(functools.partial(body, n_node, n_harm), name='residual',...  19.7 us
    unnamed x1, local copies, waits for them, and re-layouts  1.02 us

profile of v8, /device:TPU:240, one launch (start us, length us, event | category | flops | bytes accessed | tf_op | source)
XLA Modules:
  0.0 20.7 jit_solution(16962909590681801844)
XLA Ops:
  0.0 19.7 %residual.1 = f32[3,16,6144]{2,1,0:T(8,128)S(1)} custom-call(s32[16,64]{1,0:T(8,128)} %bitcast.18, s32[4,48]{1,0:T(4,128)} %bitcast.19, f32[3,16,6144]{2,1,0:T(8,128)} %bitcast.12, f32[3,16,6144]{2,1,0:T(8,128)} %bitcast.13, bf16[48,4,128,128]{3,2,1,0:T(8,128)(2,1)} %coupling_hbm.1, f32[48,128]{1,0:T(8,128)} %bitcast.14, f32[48,128]{1,0:T(8,128)} %bitcast.15, ...), custom_call_target="tpu_custom_call" | custom-call | tf_op jit(solution)/shard_map/residual/pallas_call | solution.py:479
  19.7 1.0 %copy.13 = f32[16,3,6144]{2,0,1:T(8,128)} copy(f32[16,3,6144]{2,0,1:T(8,128)S(1)} %bitcast.11) | data formatting | bytes 2359296

commit v9 on v8

--- a/solution.py
+++ b/solution.py
@@ -139,8 +139,7 @@
                 spectrum_hbm.at[:, :, at], spectrum_ref.at[:, :, at], spectrum_sem.at[c]
             )
         )
-    for copy in load_spectrum:
-        copy.start()
+    load_spectrum[0].start()
     barrier = pltpu.get_barrier_semaphore()
 
     @pl.when(~last)
@@ -154,6 +153,8 @@
         def _(neighbour=neighbour):
             pl.semaphore_signal(barrier, inc=1, device_id=(neighbour, harm), device_id_type=MESH)
 
+    for copy in load_spectrum[1:]:
+        copy.start()
     whole = [
         (halo_hbm, halo_ref),
         (synthesis_hbm, synthesis_ref),

time: 20.8 us -> 20.8 us (level)
  no operation moved by 1% of the time
where the time goes in v9:
time: 20.8 us; the launch traced here: 20.7 us
  Pallas kernels  19.7 us (95%)
  local copies, waits for them, and re-layouts  1.02 us (5%)
    pallas_call x1, Pallas kernels, local(): pl.pallas_call(functools.partial(body, n_node, n_harm), name='residual',...  19.7 us
    unnamed x1, local copies, waits for them, and re-layouts  1.02 us

profile of v9, /device:TPU:240, one launch (start us, length us, event | category | flops | bytes accessed | tf_op | source)
XLA Modules:
  0.0 20.7 jit_solution(16979278782366754400)
XLA Ops:
  0.0 19.7 %residual.1 = f32[3,16,6144]{2,1,0:T(8,128)S(1)} custom-call(s32[16,64]{1,0:T(8,128)} %bitcast.18, s32[4,48]{1,0:T(4,128)} %bitcast.19, f32[3,16,6144]{2,1,0:T(8,128)} %bitcast.12, f32[3,16,6144]{2,1,0:T(8,128)} %bitcast.13, bf16[48,4,128,128]{3,2,1,0:T(8,128)(2,1)} %coupling_hbm.1, f32[48,128]{1,0:T(8,128)} %bitcast.14, f32[48,128]{1,0:T(8,128)} %bitcast.15, ...), custom_call_target="tpu_custom_call" | custom-call | tf_op jit(solution)/shard_map/residual/pallas_call | solution.py:480
  19.7 1.0 %copy.13 = f32[16,3,6144]{2,0,1:T(8,128)} copy(f32[16,3,6144]{2,0,1:T(8,128)S(1)} %bitcast.11) | data formatting | bytes 2359296

commit v10 on v9

--- a/solution.py
+++ b/solution.py
@@ -142,16 +142,16 @@
     load_spectrum[0].start()
     barrier = pltpu.get_barrier_semaphore()
 
+    for neighbour, flag in zip(neighbours, later):
+
+        @pl.when(flag)
+        def _(neighbour=neighbour):
+            pl.semaphore_signal(barrier, inc=1, device_id=(neighbour, harm), device_id_type=MESH)
+
     @pl.when(~last)
     def _():
         for peer in peers:
             pl.semaphore_signal(barrier, inc=1, device_id=(node, peer), device_id_type=MESH)
-
-    for neighbour, flag in zip(neighbours, later):
-
-        @pl.when(flag)
-        def _(neighbour=neighbour):
-            pl.semaphore_signal(barrier, inc=1, device_id=(neighbour, harm), device_id_type=MESH)
 
     for copy in load_spectrum[1:]:
         copy.start()

time: 20.8 us -> 20.8 us (level)
  no operation moved by 1% of the time
where the time goes in v10:
time: 20.8 us; the launch traced here: 20.7 us
  Pallas kernels  19.6 us (94%)
  local copies, waits for them, and re-layouts  1.02 us (5%)
    pallas_call x1, Pallas kernels, local(): pl.pallas_call(functools.partial(body, n_node, n_harm), name='residual',...  19.6 us
    unnamed x1, local copies, waits for them, and re-layouts  1.02 us

profile of v10, /device:TPU:240, one launch (start us, length us, event | category | flops | bytes accessed | tf_op | source)
XLA Modules:
  0.0 20.7 jit_solution(1358136205891408328)
XLA Ops:
  0.0 19.6 %residual.1 = f32[3,16,6144]{2,1,0:T(8,128)S(1)} custom-call(s32[16,64]{1,0:T(8,128)} %bitcast.18, s32[4,48]{1,0:T(4,128)} %bitcast.19, f32[3,16,6144]{2,1,0:T(8,128)} %bitcast.12, f32[3,16,6144]{2,1,0:T(8,128)} %bitcast.13, bf16[48,4,128,128]{3,2,1,0:T(8,128)(2,1)} %coupling_hbm.1, f32[48,128]{1,0:T(8,128)} %bitcast.14, f32[48,128]{1,0:T(8,128)} %bitcast.15, ...), custom_call_target="tpu_custom_call" | custom-call | tf_op jit(solution)/shard_map/residual/pallas_call | solution.py:480
  19.6 1.0 %copy.13 = f32[16,3,6144]{2,0,1:T(8,128)} copy(f32[16,3,6144]{2,0,1:T(8,128)S(1)} %bitcast.11) | data formatting | bytes 2359296
